TPU v7x, 128 devices: a whole 4x4x4 slice. The times are simulated.
128 devices in a mesh: gx: 8 (over y, core), gy: 16 (over z, x).
Axes of the slice: x: 4, y: 4, z: 4, core: 2. Of those that a mesh axis runs over, the one named last changes fastest.
Arguments:
- forcing: float32 [16, 512, 2048], P(None, 'gy', 'gx'), may hold values from -6 to 6
- damping: float32 [16, 512, 2048], P(None, 'gy', 'gx'), may hold values from 0.5 to 4
- coupling: float32 [16, 16], replicated, may hold values from -1.5 to 1.5
- wind_lon: float32 [512, 2048], P('gy', 'gx'), may hold values from -0.5 to 0.5
- wind_lat: float32 [512, 2048], P('gy', 'gx'), may hold values from -0.5 to 0.5
Outputs:
- solution: float32 [16, 512, 2048], P(None, 'gy', 'gx')
- residual: float32 [16, 512, 2048], P(None, 'gy', 'gx')
All inputs are finite; a program needn't handle non-finite values.
Results may differ from a plain program's by a relative error of at most 0.0003.
Values sent between devices are 32-bit elements; how exact they have to be, the bound alone decides.
A program may use at most 64 MiB of HBM per device.

v0:
```python
import functools
import math

import jax
import jax.numpy as jnp
from jax import lax
from jax.experimental import pallas as pl
from jax.experimental.pallas import tpu as pltpu
from jax.sharding import PartitionSpec as P

ITERS = 8
COUPLE = 0.25
DIFF_LAT = 0.5
DIFF_LON = 0.5
GUARD = 1.0
MESH = pl.DeviceIdType.MESH
HI = lax.Precision.HIGHEST

MIDDLE = 9.0
RADIUS = 6.0
WIDTH = 3.0
THETA = [MIDDLE + RADIUS * math.cos(math.pi * (2 * k + 1) / (2 * ITERS)) for k in (7, 0, 4, 2, 6, 1, 5, 3)]
PAIRS = [(k, i) for k in range(ITERS + 1) for i in range(k + 1)]
GROUP = 4
HALO = 2 * ITERS
HALF = 8
WINDOWS = 3


def apply_to(coords):
    out = [None] * (len(coords) + 1)
    for k, value in enumerate(coords):
        low = THETA[k] * value if k < ITERS else value
        out[k] = low if out[k] is None else out[k] + low
        out[k + 1] = WIDTH * value
    return out


def small_solve(gram):
    first = jnp.sqrt(gram[0][0] + GUARD)
    coords = [[1.0 / first]]
    images = [[gram[i][0] * coords[0][0] for i in range(ITERS + 1)]]
    heights = []
    for j in range(ITERS):
        moved = apply_to(coords[j])
        column = []
        for i in range(j + 1):
            column.append(functools.reduce(lambda a, b: a + b, [images[i][k] * moved[k] for k in range(j + 2)]))
        left = list(moved)
        for i in range(j + 1):
            for k in range(i + 1):
                left[k] = left[k] - column[i] * coords[i][k]
        image = [
            functools.reduce(lambda a, b: a + b, [gram[r][k] * left[k] for k in range(j + 2)])
            for r in range(ITERS + 1)
        ]
        norm_sq = functools.reduce(lambda a, b: a + b, [image[k] * left[k] for k in range(j + 2)])
        subdiag = jnp.sqrt(jnp.maximum(norm_sq, 0.0) + GUARD)
        column.append(subdiag)
        heights.append(column)
        inverse = 1.0 / subdiag
        coords.append([v * inverse for v in left])
        images.append([v * inverse for v in image])
    cosines, sines, target, rotated = [], [], [first], []
    for j in range(ITERS):
        column = list(heights[j])
        for e in range(j):
            upper, lower = column[e], column[e + 1]
            column[e] = cosines[e] * upper + sines[e] * lower
            column[e + 1] = cosines[e] * lower - sines[e] * upper
        upper, lower = column[j], column[j + 1]
        radius = jnp.sqrt(upper * upper + lower * lower)
        inverse = 1.0 / radius
        cosine, sine = upper * inverse, lower * inverse
        column[j] = radius
        kept = target[j]
        target[j] = cosine * kept
        target.append(-sine * kept)
        cosines.append(cosine)
        sines.append(sine)
        rotated.append(column)
    weights = [None] * ITERS
    for j in reversed(range(ITERS)):
        value = target[j]
        for later in range(j + 1, ITERS):
            value = value - rotated[later][j] * weights[later]
        weights[j] = value / rotated[j][j]
    answer = [None] * ITERS
    for j in range(ITERS):
        for k in range(j + 1):
            term = weights[j] * coords[j][k]
            answer[k] = term if answer[k] is None else answer[k] + term
    return answer, apply_to(answer)


def distance(n, o):
    return min(o, n - o)


def peers(nx, ny):
    inner = 4 if ny % 4 == 0 else 1
    offsets = [(a, b) for a in range(nx) for b in range(ny) if (a, b) != (0, 0)]

    def hops(offset):
        a, b = offset
        return distance(nx // 2 or 1, a // 2) + distance(inner, b % inner) + distance(ny // inner, b // inner)

    return sorted(offsets, key=lambda offset: (-hops(offset), offset))


def kernel(nx, ny, f_hbm, d_hbm, c_ref, wl_hbm, wa_hbm, sol_hbm, res_hbm,
           basis, diag, coef, kxs, block, band, own, near_lat, near_lon, own_w, near_lat_w, near_lon_w, corner_out, corner_in,
           gram_acc, mine, slots, splats, outs,
           load_sem, wind_sem, out_sem, lat_send, lat_recv, lon_send, lon_recv, cor_send, cor_recv, red_sem, known):
    channels, lat, lon = f_hbm.shape
    total = nx * ny
    f32, bf16 = jnp.float32, jnp.bfloat16
    ix, iy = lax.axis_index("gx"), lax.axis_index("gy")
    me = ix * ny + iy
    east, west = lax.rem(ix + 1, nx), lax.rem(ix + nx - 1, nx)
    scale = 1.0 / WIDTH
    size = GROUP * channels
    edge = HALO
    rows_all = lat + 2 * HALO

    winds = [pltpu.make_async_copy(wl_hbm, own_w.at[0], wind_sem.at[0]), pltpu.make_async_copy(wa_hbm, own_w.at[1], wind_sem.at[1])]
    batches = (lat // HALF - 1, 0, lat // HALF - 2, 1)
    for b in batches:
        for r in range(HALF * b, HALF * b + HALF):
            for q, src in enumerate((f_hbm, d_hbm)):
                pltpu.make_async_copy(src.at[:, r, :], own.at[r, pl.ds(q * channels, channels), :], load_sem.at[b]).start()
    for copy in winds:
        copy.start()

    barrier = pltpu.get_barrier_semaphore()

    def greet(sem, a, b):
        pl.semaphore_signal(sem, inc=1, device_id=(lax.rem(ix + a, nx), lax.rem(iy + b, ny)), device_id_type=MESH)

    greeted = [(1, 0), (nx - 1, 0), (0, 1), (0, ny - 1), (1, 1), (1, ny - 1), (nx - 1, 1), (nx - 1, ny - 1)]
    greeted += [(a, 0) for a in range(2, nx - 1)] + [(0, b) for b in range(2, ny - 1)]
    for a, b in greeted:
        greet(barrier, a, b)

    def spread(n):
        row = lax.broadcasted_iota(jnp.int32, (n, channels), 0)
        col = lax.broadcasted_iota(jnp.int32, (n, channels), 1)
        return jnp.where(lax.rem(row, channels) == col, 1.0, 0.0).astype(f32)

    wide = lax.dot_general(spread(size), c_ref[...], (((1,), (0,)), ((), ())), precision=HI, preferred_element_type=f32)
    wide = lax.dot_general(wide, spread(3 * size), (((1,), (1,)), ((), ())), precision=HI,
                           preferred_element_type=f32) * (COUPLE * scale)
    down = lax.broadcasted_iota(jnp.int32, (size, 3 * size), 0)
    across = lax.broadcasted_iota(jnp.int32, (size, 3 * size), 1)
    high = wide.astype(bf16).astype(f32)
    wide = jnp.where(across < 2 * size, high, wide - high)
    block[...] = jnp.where(down // channels == lax.rem(across, size) // channels, wide, 0.0).astype(bf16)
    down = lax.broadcasted_iota(jnp.int32, (256, 256), 0)
    across = lax.broadcasted_iota(jnp.int32, (256, 256), 1)
    shift = lax.rem(down, 128) - lax.rem(across, 128)
    sums = jnp.where((shift == 1) | (shift == -1), 1.0, 0.0)
    slopes = jnp.where(shift == 1, 8.0, 0.0) + jnp.where(shift == -1, -8.0, 0.0)
    slopes = slopes + jnp.where(shift == 2, -1.0, 0.0) + jnp.where(shift == -2, 1.0, 0.0)
    band[...] = jnp.where(across < 128, sums, slopes).astype(bf16)
    row_pos = (lax.broadcasted_iota(jnp.int32, (rows_all, 128), 0) + (iy * lat - edge)).astype(f32)
    phi = -math.pi / 2 + (row_pos + 0.5) * (math.pi / (lat * ny))
    kxs[...] = (DIFF_LON * scale) / (jnp.cos(phi) ** 2 + 0.1)

    @pl.when(iy == 0)
    def _():
        near_lat[0] = jnp.zeros(near_lat.shape[1:], f32)
        near_lat_w[0] = jnp.zeros(near_lat_w.shape[1:], f32)
        corner_in[0] = jnp.zeros(corner_in.shape[1:], f32)
        corner_in[1] = jnp.zeros(corner_in.shape[1:], f32)

    @pl.when(iy == ny - 1)
    def _():
        near_lat[1] = jnp.zeros(near_lat.shape[1:], f32)
        near_lat_w[1] = jnp.zeros(near_lat_w.shape[1:], f32)
        corner_in[2] = jnp.zeros(corner_in.shape[1:], f32)
        corner_in[3] = jnp.zeros(corner_in.shape[1:], f32)

    pl.semaphore_wait(barrier, len(greeted))

    def lat_copies(side, c):
        first = HALF * (1 - c) if side == 0 else HALF * c
        base = lat - HALO if side == 0 else 0
        to = (ix, iy + 1) if side == 0 else (ix, iy - 1)
        kept = (first, HALF, 0, 2 * channels)
        if c == 0:
            parts = [kept]
        elif side == 0:
            parts = [(first + 2, HALF - 2, 0, 2 * channels), (first, 2, 0, channels)]
        else:
            parts = [(first, HALF - 2, 0, 2 * channels), (first + HALF - 2, 2, 0, channels)]
        out = []
        for n, (start, count, sub, subs) in enumerate(parts):
            out.append(pltpu.make_async_remote_copy(
                src_ref=own.at[pl.ds(base + start, count), pl.ds(sub, subs), :],
                dst_ref=near_lat.at[side, pl.ds(start, count), pl.ds(sub, subs), :],
                send_sem=lat_send.at[side, c, n], recv_sem=lat_recv.at[side, c, n], device_id=to, device_id_type=MESH))
        out.append(pltpu.make_async_remote_copy(
            src_ref=own_w.at[:, pl.ds(base + first, HALF), :], dst_ref=near_lat_w.at[side, :, pl.ds(first, HALF), :],
            send_sem=lat_send.at[side, c, 2], recv_sem=lat_recv.at[side, c, 2], device_id=to, device_id_type=MESH))
        return out

    def corner_copy(side, ew, c):
        slot = 2 * side + ew
        tile = 1 - c if side == 0 else c
        return pltpu.make_async_remote_copy(
            src_ref=corner_out.at[slot, tile], dst_ref=corner_in.at[slot, tile],
            send_sem=cor_send.at[slot, c], recv_sem=cor_recv.at[slot, c],
            device_id=(east if ew == 0 else west, iy + 1 if side == 0 else iy - 1), device_id_type=MESH)

    def lon_copies(ew):
        cut = pl.ds(lon - 128, 128) if ew == 0 else pl.ds(0, 128)
        to = (east if ew == 0 else west, iy)
        return [
            pltpu.make_async_remote_copy(
                src_ref=own.at[:, :, cut], dst_ref=near_lon.at[ew], send_sem=lon_send.at[ew, 0], recv_sem=lon_recv.at[ew, 0],
                device_id=to, device_id_type=MESH),
            pltpu.make_async_remote_copy(
                src_ref=own_w.at[:, :, cut], dst_ref=near_lon_w.at[ew], send_sem=lon_send.at[ew, 1], recv_sem=lon_recv.at[ew, 1],
                device_id=to, device_id_type=MESH),
        ]

    def has(side):
        return iy < ny - 1 if side == 0 else iy > 0

    def from_side(side):
        return iy > 0 if side == 0 else iy < ny - 1

    lane = lax.broadcasted_iota(jnp.int32, (2 * channels, 128), 1)
    lane8 = lax.broadcasted_iota(jnp.int32, (8, 128), 1)

    def turn(x, n):
        n = n % 128
        return pltpu.roll(x, n, 1) if n else x

    def pack_corner(side, ew, c):
        slot = 2 * side + ew
        tile = 1 - c if side == 0 else c
        base = (lat - HALO if side == 0 else 0) + HALF * tile
        cut = slice(lon - 128, lon) if ew == 0 else slice(0, 128)
        start = 112 if ew == 0 else 0
        packed = turn(own[base, :, cut], -start)
        for j in range(1, HALF):
            packed = jnp.where((lane >= 16 * j) & (lane < 16 * j + 16), turn(own[base + j, :, cut], 16 * j - start), packed)
        corner_out[slot, tile, 0:2 * channels, :] = packed
        corner_out[slot, tile, 2 * channels:2 * channels + 8, :] = jnp.where(
            lane8 < 16, turn(own_w[0, base:base + 8, cut], -start), turn(own_w[1, base:base + 8, cut], 16 - start))

    def loaded(b):
        part = own.at[pl.ds(HALF * b, HALF)]
        pltpu.make_async_copy(part, part, load_sem.at[b]).wait()

    for copy in winds:
        copy.wait()
    for c in range(2):
        for side in range(2):
            loaded(batches[2 * c + side])

            @pl.when(has(side))
            def _():
                copies = lat_copies(side, c)
                copies[0].start()
                for ew in range(2):
                    pack_corner(side, ew, c)
                    corner_copy(side, ew, c).start()
                for copy in copies[1:]:
                    if copy is not None and not (c == 0 and copy is copies[0]):
                        copy.start()

    for ew in range(2):
        for copy in lon_copies(ew):
            copy.start()
    for b in range(1, ny):
        greet(known, 0, b)

    def place_coef(e0, wl, wa, inside):
        kx = kxs[pl.ds(e0, 8), :]
        for t in range(WINDOWS):
            cut = slice(128 * t, 128 * t + 128)
            l, a = wl[t] * (scale / 12.0), wa[t] * (scale / 12.0)
            planes = [-kx, l, 8.0 * a - DIFF_LAT * scale, -8.0 * a - DIFF_LAT * scale, a]
            for q, plane in enumerate(planes):
                if inside is not None:
                    plane = plane * inside
                for j in range(8):
                    coef[e0 + j, q:q + 1, cut] = plane[j:j + 1, :]

    def place_row(e, pieces):
        centre = (1.0 + 2.0 * DIFF_LAT) * scale - 2.0 * coef[e, 0:1, 0:128]
        for t in range(WINDOWS):
            cut = slice(128 * t, 128 * t + 128)
            basis[0, e, :, cut] = pieces[t][0:channels]
            diag[e, :, cut] = pieces[t][channels:] * scale + centre

    def cuts(lanes, a, b, w, e):
        return (turn(jnp.where(lanes >= 112, w, a), 16), turn(jnp.where(lanes >= 64, a, b), 64),
                turn(jnp.where(lanes >= 16, b, e), 112))

    for ew in range(2):
        for copy in lon_copies(ew):
            copy.wait_recv()
    for n in range(lat // 8):
        at = slice(8 * n, 8 * n + 8)
        wl, wa = (cuts(lane8, own_w[q, at, 0:128], own_w[q, at, 128:256], near_lon_w[0, q, at, :], near_lon_w[1, q, at, :])
                  for q in range(2))
        place_coef(edge + 8 * n, wl, wa, None)

    def place_own(r, _):
        place_row(edge + r, cuts(lane, own[r, :, 0:128], own[r, :, 128:256], near_lon[0, r], near_lon[1, r]))
        return 0

    lax.fori_loop(0, lat, place_own, 0)

    def place_halo(side, c):
        first = HALF * (1 - c) if side == 0 else HALF * c
        tile = 1 - c if side == 0 else c
        e0 = first if side == 0 else edge + lat + first
        inside = jnp.where(from_side(side), 1.0, 0.0).astype(f32)

        @pl.when(from_side(side))
        def _():
            for copy in lat_copies(side, c):
                copy.wait_recv()
            for ew in range(2):
                corner_copy(side, ew, c).wait_recv()

        def pair(q):
            a, b = near_lat_w[side, q, first:first + 8, 0:128], near_lat_w[side, q, first:first + 8, 128:256]
            w = corner_in[2 * side, tile, 2 * channels:2 * channels + 8, :]
            e = corner_in[2 * side + 1, tile, 2 * channels:2 * channels + 8, :]
            return (jnp.where(lane8 < 16, turn(w, -16 * q), turn(a, 16)), turn(jnp.where(lane8 >= 64, a, b), 64),
                    jnp.where(lane8 >= 112, turn(e, 112 - 16 * q), turn(b, 112)))

        place_coef(e0, pair(0), pair(1), inside)
        for j in range(HALF):
            a, b = near_lat[side, first + j, :, 0:128], near_lat[side, first + j, :, 128:256]
            w, e = corner_in[2 * side, tile, 0:2 * channels, :], corner_in[2 * side + 1, tile, 0:2 * channels, :]
            place_row(e0 + j, (
                jnp.where(lane < 16, turn(w, -16 * j), turn(a, 16)), turn(jnp.where(lane >= 64, a, b), 64),
                jnp.where(lane >= 112, turn(e, 112 - 16 * j), turn(b, 112))))

    def advance(k, starts):
        theta = jnp.float32(THETA[0] * scale)
        for i in range(1, ITERS):
            theta = jnp.where(k == i, jnp.float32(THETA[i] * scale), theta)
        for e0 in starts:
            for g in range(HALF // GROUP):
                picked = [e0 + GROUP * g + j for j in range(GROUP)]
                stack = jnp.concatenate([basis[k, e] for e in picked], axis=0)
                high = stack.astype(bf16)
                low = (stack - high.astype(f32)).astype(bf16)
                mixed = lax.dot_general(block[...], jnp.concatenate([high, low, high], axis=0), (((1,), (0,)), ((), ())),
                                        preferred_element_type=f32)
                sides = jnp.concatenate(
                    [jnp.concatenate([high[:, 128 * t:128 * t + 128], low[:, 128 * t:128 * t + 128]], axis=1)
                     for t in range(WINDOWS)], axis=0)
                moved = lax.dot_general(sides, band[...], (((1,), (0,)), ((), ())), preferred_element_type=f32)
                for j, e in enumerate(picked):
                    for t in range(WINDOWS):
                        cut = slice(128 * t, 128 * t + 128)
                        at = slice(size * t + channels * j, size * t + channels * (j + 1))

                        def weight(q):
                            return coef[e, q:q + 1, cut]

                        value = (diag[e, :, cut] - theta) * basis[k, e, :, cut] + mixed[channels * j:channels * (j + 1), cut]
                        value = value + (coef[e, 0:1, 0:128] * moved[at, 0:128] + weight(1) * moved[at, 128:256])
                        value = value + weight(2) * basis[k, e + 1, :, cut] + weight(3) * basis[k, e - 1, :, cut]
                        value = value + weight(4) * (basis[k, e - 2, :, cut] - basis[k, e + 2, :, cut])
                        basis[k + 1, e, :, cut] = value

    def interior(k, _):
        def some(n, _):
            advance(k, (edge + 2 + 2 * k + HALF * n, edge + lat - 2 - HALF - 2 * k - HALF * n))
            return 0

        lax.fori_loop(0, jnp.where(k < 3, 2, 1), some, 0)
        return 0

    def dots(lo, hi, spans):
        pairs = [(k, i) for k, i in PAIRS if lo <= k <= hi]

        def one(t, _):
            cut = pl.ds(pl.multiple_of(t * 128, 128), 128)
            acc = (jnp.zeros((8, 128), f32),) * len(pairs)
            for start, stop in spans:
                def part(e, acc):
                    acc = list(acc)
                    for h in range(channels // 8):
                        x = [basis[k, e, 8 * h:8 * h + 8, cut] for k in range(hi + 1)]
                        for n, (k, i) in enumerate(pairs):
                            acc[n] = acc[n] + x[k] * x[i]
                    return tuple(acc)

                acc = lax.fori_loop(start, stop, part, acc)
            low = jnp.where(t == 1, 32, 16)
            kept = (lane8 >= low) & (lane8 < 128 - low)
            for n, (k, i) in enumerate(pairs):
                at = k * (k + 1) // 2 + i
                gram_acc[at] = gram_acc[at] + jnp.where(kept, acc[n], 0.0)
            return 0

        lax.fori_loop(0, WINDOWS, one, 0)

    gram_acc[...] = jnp.zeros(gram_acc.shape, f32)
    lax.fori_loop(0, ITERS - 1, interior, 0)
    ready = ITERS // 2
    for c in range(2):
        for side in range(2):
            place_halo(side, c)

        def wedge(k, _):
            low = edge - HALF * (c + 1) + 2 + 2 * k
            advance(k, (low, rows_all - HALF - low))
            return 0

        lax.fori_loop(0, ITERS, wedge, 0)
        if c == 0:
            dots(0, ready, ((edge, edge + lat),))
            dots(ready + 1, ITERS, ((edge + HALF, edge + lat - HALF),))
    dots(ready + 1, ITERS, ((edge, edge + HALF), (edge + lat - HALF, edge + lat)))

    pl.semaphore_wait(known, ny - 1)
    sums = jnp.concatenate(
        [jnp.sum(gram_acc[n], axis=0, keepdims=True) for n in range(len(PAIRS))]
        + [jnp.zeros((128 - len(PAIRS), 128), f32)], axis=0)
    flat = lax.dot_general(jnp.ones((8, 128), f32), sums, (((1,), (1,)), ((), ())), precision=HI,
                           preferred_element_type=f32)
    mine[...] = flat[0:1, :]
    slots[total - 1] = flat[0:1, :]

    for n, (a, b) in enumerate(peers(nx, ny)):
        pltpu.make_async_remote_copy(
            src_ref=mine, dst_ref=slots.at[n], send_sem=red_sem.at[0], recv_sem=red_sem.at[1],
            device_id=(lax.rem(ix + a, nx), lax.rem(iy + b, ny)), device_id_type=MESH).start()
    arrived = slots.at[pl.ds(0, total - 1)]
    pltpu.make_async_copy(arrived, arrived, red_sem.at[1]).wait()
    pltpu.make_async_copy(arrived, arrived, red_sem.at[0]).wait()
    parts = [slots[n] for n in range(4)]
    for n in range(4, total):
        parts[n % 4] = parts[n % 4] + slots[n]
    whole = (parts[0] + parts[1]) + (parts[2] + parts[3])
    gram = [[None] * (ITERS + 1) for _ in range(ITERS + 1)]
    for n, (k, i) in enumerate(PAIRS):
        gram[k][i] = gram[i][k] = jnp.broadcast_to(whole[:, n:n + 1], (8, 128))
    answer, applied = small_solve(gram)
    for k in range(ITERS):
        splats[k] = answer[k]
    for k in range(ITERS + 1):
        splats[ITERS + k] = applied[k]

    def finish(r, _):
        for h in range(channels // 8):
            sub = slice(8 * h, 8 * h + 8)
            best, rest = [], []
            for t in range(WINDOWS):
                cut = slice(128 * t, 128 * t + 128)
                x = basis[0, edge + r, sub, cut]
                up = splats[0] * x
                down = x - splats[ITERS] * x
                for k in range(1, ITERS + 1):
                    x = basis[k, edge + r, sub, cut]
                    if k < ITERS:
                        up = up + splats[k] * x
                    down = down - splats[ITERS + k] * x
                best.append(up)
                rest.append(down)
            for q, (a, b, c) in enumerate((best, rest)):
                b = turn(b, 64)
                outs[q, r, sub, 0:128] = jnp.where(lane8 < 96, turn(a, 112), b)
                outs[q, r, sub, 128:256] = jnp.where(lane8 < 32, b, turn(c, 16))
        return 0

    lax.fori_loop(0, lat, finish, 0)
    for c in range(channels):
        for q, dst in enumerate((sol_hbm, res_hbm)):
            pltpu.make_async_copy(outs.at[q, :, c, :], dst.at[c], out_sem.at[q]).start()
    for ew in range(2):
        for copy in lon_copies(ew):
            copy.wait_send()
    for side in range(2):
        @pl.when(has(side))
        def _():
            for c in range(2):
                for copy in lat_copies(side, c):
                    copy.wait_send()
                for ew in range(2):
                    corner_copy(side, ew, c).wait_send()
    for q, dst in enumerate((sol_hbm, res_hbm)):
        pltpu.make_async_copy(dst, dst, out_sem.at[q]).wait()


def solution(mesh):
    nx, ny = mesh.shape["gx"], mesh.shape["gy"]

    def per_device(forcing, damping, coupling, wind_lon, wind_lat):
        channels, lat, lon = forcing.shape
        f32 = jnp.float32
        vmem = pl.BlockSpec(memory_space=pltpu.VMEM)
        hbm = pl.BlockSpec(memory_space=pl.ANY)
        dma = pltpu.SemaphoreType.DMA
        shape = jax.ShapeDtypeStruct((channels, lat, lon), f32)
        rows_all, lanes = lat + 2 * HALO, 128 * WINDOWS
        packed = 2 * channels + 8
        return pl.pallas_call(
            functools.partial(kernel, nx, ny),
            out_shape=(shape, shape),
            in_specs=[hbm, hbm, vmem, hbm, hbm],
            out_specs=(hbm, hbm),
            scratch_shapes=[
                pltpu.VMEM((ITERS + 1, rows_all, channels, lanes), f32),
                pltpu.VMEM((rows_all, channels, lanes), f32),
                pltpu.VMEM((rows_all, 8, lanes), f32),
                pltpu.VMEM((rows_all, 128), f32),
                pltpu.VMEM((GROUP * channels, 3 * GROUP * channels), jnp.bfloat16),
                pltpu.VMEM((256, 256), jnp.bfloat16),
                pltpu.VMEM((lat, 2 * channels, lon), f32),
                pltpu.VMEM((2, HALO, 2 * channels, lon), f32),
                pltpu.VMEM((2, lat, 2 * channels, 128), f32),
                pltpu.VMEM((2, lat, lon), f32),
                pltpu.VMEM((2, 2, HALO, lon), f32),
                pltpu.VMEM((2, 2, lat, 128), f32),
                pltpu.VMEM((4, 2, packed, 128), f32),
                pltpu.VMEM((4, 2, packed, 128), f32),
                pltpu.VMEM((len(PAIRS), 8, 128), f32),
                pltpu.VMEM((1, 128), f32),
                pltpu.VMEM((nx * ny, 1, 128), f32),
                pltpu.VMEM((2 * ITERS + 1, 8, 128), f32),
                pltpu.VMEM((2, lat, channels, lon), f32),
                dma((lat // HALF,)), dma((2,)), dma((2,)),
                dma((2, 2, 3)), dma((2, 2, 3)), dma((2, 2)), dma((2, 2)), dma((4, 2)), dma((4, 2)), dma((2,)),
                pltpu.SemaphoreType.REGULAR,
            ],
            compiler_params=pltpu.CompilerParams(
                collective_id=0, has_side_effects=True, vmem_limit_bytes=63 * 1024 * 1024),
        )(forcing, damping, coupling, wind_lon, wind_lat)

    return jax.shard_map(
        per_device,
        mesh=mesh,
        in_specs=(P(None, "gy", "gx"), P(None, "gy", "gx"), P(), P("gy", "gx"), P("gy", "gx")),
        out_specs=(P(None, "gy", "gx"), P(None, "gy", "gx")),
        check_vma=False,
    )
```

profile of v0, /device:TPU:1, one launch (start us, length us, event | category | flops | bytes accessed | tf_op | source)
XLA Modules:
  0.0 59.1 jit_solution(15365856738909801663)
XLA Ops:
  0.6 55.7 %shard_map.68 = (f32[16,32,256]{2,1,0:T(8,128)}, f32[16,32,256]{2,1,0:T(8,128)}) custom-call(f32[16,32,256]{2,1,0:T(8,128)} %f_hbm.1, f32[16,32,256]{2,1,0:T(8,128)} %d_hbm.1, f32[16,16]{1,0:T(8,128)} %c_ref.1, f32[32,256]{1,0:T(8,128)} %wl_hbm.1, f32[32,256]{1,0:T(8,128)} %wa_hbm.1), custom_call_target="tpu_custom_call" | custom-call | tf_op jit(solution)/shard_map/pallas_call | solution.py:509
  56.3 0.0 copy-start
  56.3 1.9 %copy.9 = f32[16,32,256]{2,1,0:T(8,128)} copy(f32[16,32,256]{2,1,0:T(8,128)} %get-tuple-element.4) | data formatting | bytes 1048576
  58.3 0.0 copy-done
  58.3 0.8 %copy.10 = f32[16,32,256]{2,1,0:T(8,128)} copy(f32[16,32,256]{2,1,0:T(8,128)S(1)} %copy-done) | data formatting | bytes 1048576
Async XLA Ops:
  56.3 2.0 %copy-start = (f32[16,32,256]{2,1,0:T(8,128)S(1)}, f32[16,32,256]{2,1,0:T(8,128)}, u32[]{:S(2)}) copy-start(f32[16,32,256]{2,1,0:T(8,128)} %get-tuple-element.5) | copy-start | bytes 1572868
where the time goes:
time: 59.2 us; the launch traced here: 59.1 us
  Pallas kernels  55.7 us (94%)
  local copies, waits for them, and re-layouts  2.74 us (5%)
  between operations  0.65 us (1%)
    pallas_call x1, Pallas kernels, per_device(): pl.pallas_call(functools.partial(kernel, nx, ny), out_shape=(shape, shape...  55.7 us
    unnamed x4, local copies, waits for them, and re-layouts  2.74 us

commit v1 on v0

v1 whole, which is shorter than its diff:
```python
import functools
import math

import jax
import jax.numpy as jnp
from jax import lax
from jax.experimental import pallas as pl
from jax.experimental.pallas import tpu as pltpu
from jax.sharding import PartitionSpec as P

ITERS = 8
COUPLE = 0.25
DIFF_LAT = 0.5
DIFF_LON = 0.5
GUARD = 1.0
MESH = pl.DeviceIdType.MESH
HI = lax.Precision.HIGHEST

MIDDLE = 9.0
RADIUS = 6.0
WIDTH = 3.0
THETA = [MIDDLE + RADIUS * math.cos(math.pi * (2 * k + 1) / (2 * ITERS)) for k in (7, 0, 4, 2, 6, 1, 5, 3)]
PAIRS = [(k, i) for k in range(ITERS + 1) for i in range(k + 1)]
GROUP = 4
HALO = 2 * ITERS
HALF = 8
WINDOWS = 3


def apply_to(coords):
    out = [None] * (len(coords) + 1)
    for k, value in enumerate(coords):
        low = THETA[k] * value if k < ITERS else value
        out[k] = low if out[k] is None else out[k] + low
        out[k + 1] = WIDTH * value
    return out


def small_solve(gram):
    first = jnp.sqrt(gram[0][0] + GUARD)
    coords = [[1.0 / first]]
    images = [[gram[i][0] * coords[0][0] for i in range(ITERS + 1)]]
    heights = []
    for j in range(ITERS):
        moved = apply_to(coords[j])
        column = []
        for i in range(j + 1):
            column.append(functools.reduce(lambda a, b: a + b, [images[i][k] * moved[k] for k in range(j + 2)]))
        left = list(moved)
        for i in range(j + 1):
            for k in range(i + 1):
                left[k] = left[k] - column[i] * coords[i][k]
        image = [
            functools.reduce(lambda a, b: a + b, [gram[r][k] * left[k] for k in range(j + 2)])
            for r in range(ITERS + 1)
        ]
        norm_sq = functools.reduce(lambda a, b: a + b, [image[k] * left[k] for k in range(j + 2)])
        subdiag = jnp.sqrt(jnp.maximum(norm_sq, 0.0) + GUARD)
        column.append(subdiag)
        heights.append(column)
        inverse = 1.0 / subdiag
        coords.append([v * inverse for v in left])
        images.append([v * inverse for v in image])
    cosines, sines, target, rotated = [], [], [first], []
    for j in range(ITERS):
        column = list(heights[j])
        for e in range(j):
            upper, lower = column[e], column[e + 1]
            column[e] = cosines[e] * upper + sines[e] * lower
            column[e + 1] = cosines[e] * lower - sines[e] * upper
        upper, lower = column[j], column[j + 1]
        radius = jnp.sqrt(upper * upper + lower * lower)
        inverse = 1.0 / radius
        cosine, sine = upper * inverse, lower * inverse
        column[j] = radius
        kept = target[j]
        target[j] = cosine * kept
        target.append(-sine * kept)
        cosines.append(cosine)
        sines.append(sine)
        rotated.append(column)
    weights = [None] * ITERS
    for j in reversed(range(ITERS)):
        value = target[j]
        for later in range(j + 1, ITERS):
            value = value - rotated[later][j] * weights[later]
        weights[j] = value / rotated[j][j]
    answer = [None] * ITERS
    for j in range(ITERS):
        for k in range(j + 1):
            term = weights[j] * coords[j][k]
            answer[k] = term if answer[k] is None else answer[k] + term
    return answer, apply_to(answer)


def distance(n, o):
    return min(o, n - o)


def peers(nx, ny):
    inner = 4 if ny % 4 == 0 else 1
    offsets = [(a, b) for a in range(nx) for b in range(ny) if (a, b) != (0, 0)]

    def hops(offset):
        a, b = offset
        return distance(nx // 2 or 1, a // 2) + distance(inner, b % inner) + distance(ny // inner, b // inner)

    return sorted(offsets, key=lambda offset: (-hops(offset), offset))


def kernel(nx, ny, f_hbm, d_hbm, c_ref, wl_hbm, wa_hbm, sol_hbm, res_hbm,
           even, odd, diag, coef, kxs, block, band, own, near_lat, own_w, near_lat_w, packed, near_lon, near_corner,
           gram_acc, mine, slots, splats, outs,
           load_sem, wind_sem, out_sem, lat_send, lat_recv, lon_send, lon_recv, cor_send, cor_recv, red_sem, known):
    channels, lat, lon = f_hbm.shape
    both = 2 * channels
    total = nx * ny
    f32, bf16 = jnp.float32, jnp.bfloat16
    ix, iy = lax.axis_index("gx"), lax.axis_index("gy")
    east, west = lax.rem(ix + 1, nx), lax.rem(ix + nx - 1, nx)
    scale = 1.0 / WIDTH
    size = GROUP * channels
    edge = HALO
    rows_all = lat + 2 * HALO
    tiles = lat // HALF

    def field(k):
        return even.at[k // 2] if k % 2 == 0 else odd.at[k // 2]

    barrier = pltpu.get_barrier_semaphore()

    def greet(sem, a, b):
        pl.semaphore_signal(sem, inc=1, device_id=(lax.rem(ix + a, nx), lax.rem(iy + b, ny)), device_id_type=MESH)

    greeted = [(1, 1), (1, ny - 1), (nx - 1, 1), (nx - 1, ny - 1), (0, 1), (0, ny - 1), (1, 0), (nx - 1, 0)]
    greeted += [(a, 0) for a in range(2, nx - 1)] + [(0, b) for b in range(2, ny - 1)]
    for a, b in greeted:
        greet(barrier, a, b)

    winds = [pltpu.make_async_copy(wl_hbm, own_w.at[0], wind_sem.at[0]), pltpu.make_async_copy(wa_hbm, own_w.at[1], wind_sem.at[1])]
    for copy in winds:
        copy.start()
    for c in range(channels):
        for q, src in enumerate((f_hbm, d_hbm)):
            pltpu.make_async_copy(src.at[c], own.at[:, q * channels + c, :], load_sem.at[q]).start()

    def spread(n):
        row = lax.broadcasted_iota(jnp.int32, (n, channels), 0)
        col = lax.broadcasted_iota(jnp.int32, (n, channels), 1)
        return jnp.where(lax.rem(row, channels) == col, 1.0, 0.0).astype(f32)

    wide = lax.dot_general(spread(size), c_ref[...], (((1,), (0,)), ((), ())), precision=HI, preferred_element_type=f32)
    wide = lax.dot_general(wide, spread(3 * size), (((1,), (1,)), ((), ())), precision=HI,
                           preferred_element_type=f32) * (COUPLE * scale)
    down = lax.broadcasted_iota(jnp.int32, (size, 3 * size), 0)
    across = lax.broadcasted_iota(jnp.int32, (size, 3 * size), 1)
    high = wide.astype(bf16).astype(f32)
    wide = jnp.where(across < 2 * size, high, wide - high)
    block[...] = jnp.where(down // channels == lax.rem(across, size) // channels, wide, 0.0).astype(bf16)
    down = lax.broadcasted_iota(jnp.int32, (256, 256), 0)
    across = lax.broadcasted_iota(jnp.int32, (256, 256), 1)
    shift = lax.rem(down, 128) - lax.rem(across, 128)
    sums = jnp.where((shift == 1) | (shift == -1), 1.0, 0.0)
    slopes = jnp.where(shift == 1, 8.0, 0.0) + jnp.where(shift == -1, -8.0, 0.0)
    slopes = slopes + jnp.where(shift == 2, -1.0, 0.0) + jnp.where(shift == -2, 1.0, 0.0)
    band[...] = jnp.where(across < 128, sums, slopes).astype(bf16)
    row_pos = (lax.broadcasted_iota(jnp.int32, (rows_all, 128), 0) + (iy * lat - edge)).astype(f32)
    phi = -math.pi / 2 + (row_pos + 0.5) * (math.pi / (lat * ny))
    kxs[...] = (DIFF_LON * scale) / (jnp.cos(phi) ** 2 + 0.1)
    gram_acc[...] = jnp.zeros(gram_acc.shape, f32)

    @pl.when(iy == 0)
    def _():
        near_lat[0] = jnp.zeros(near_lat.shape[1:], f32)
        near_lat_w[0] = jnp.zeros(near_lat_w.shape[1:], f32)
        near_corner[0] = jnp.zeros(near_corner.shape[1:], f32)
        near_corner[1] = jnp.zeros(near_corner.shape[1:], f32)

    @pl.when(iy == ny - 1)
    def _():
        near_lat[1] = jnp.zeros(near_lat.shape[1:], f32)
        near_lat_w[1] = jnp.zeros(near_lat_w.shape[1:], f32)
        near_corner[2] = jnp.zeros(near_corner.shape[1:], f32)
        near_corner[3] = jnp.zeros(near_corner.shape[1:], f32)

    def lat_copies(side, c):
        first = HALF * (1 - c) if side == 0 else HALF * c
        base = lat - HALO if side == 0 else 0
        to = (ix, iy + 1) if side == 0 else (ix, iy - 1)
        if c == 0:
            parts = [(first, HALF, 0, both)]
        elif side == 0:
            parts = [(first + 2, HALF - 2, 0, both), (first, 2, 0, channels)]
        else:
            parts = [(first, HALF - 2, 0, both), (first + HALF - 2, 2, 0, channels)]
        out = []
        for n, (start, count, sub, subs) in enumerate(parts):
            out.append(pltpu.make_async_remote_copy(
                src_ref=own.at[pl.ds(base + start, count), pl.ds(sub, subs), :],
                dst_ref=near_lat.at[side, pl.ds(start, count), pl.ds(sub, subs), :],
                send_sem=lat_send.at[side, c, n], recv_sem=lat_recv.at[side, c, n], device_id=to, device_id_type=MESH))
        out.append(pltpu.make_async_remote_copy(
            src_ref=own_w.at[:, pl.ds(base + first, HALF), :], dst_ref=near_lat_w.at[side, :, pl.ds(first, HALF), :],
            send_sem=lat_send.at[side, c, 2], recv_sem=lat_recv.at[side, c, 2], device_id=to, device_id_type=MESH))
        return out

    def tile_of(side, c):
        return 1 - c if side == 0 else c

    def corner_copy(side, ew, c):
        slot, tile = 2 * side + ew, tile_of(side, c)
        return pltpu.make_async_remote_copy(
            src_ref=packed.at[ew, tile + (tiles - 2 if side == 0 else 0)], dst_ref=near_corner.at[slot, tile],
            send_sem=cor_send.at[slot, c], recv_sem=cor_recv.at[slot, c],
            device_id=(east if ew == 0 else west, iy + 1 if side == 0 else iy - 1), device_id_type=MESH)

    def lon_copy(ew):
        return pltpu.make_async_remote_copy(
            src_ref=packed.at[ew], dst_ref=near_lon.at[ew], send_sem=lon_send.at[ew], recv_sem=lon_recv.at[ew],
            device_id=(east if ew == 0 else west, iy), device_id_type=MESH)

    def has(side):
        return iy < ny - 1 if side == 0 else iy > 0

    def from_side(side):
        return iy > 0 if side == 0 else iy < ny - 1

    lane = lax.broadcasted_iota(jnp.int32, (both, 128), 1)
    lane8 = lax.broadcasted_iota(jnp.int32, (8, 128), 1)

    def turn(x, n):
        n = n % 128
        return pltpu.roll(x, n, 1) if n else x

    def pack(n, _):
        for ew in range(2):
            cut = slice(lon - 128, lon) if ew == 0 else slice(0, 128)
            start = 112 if ew == 0 else 0
            base = HALF * n
            strip = turn(own[base, :, cut], -start)
            for j in range(1, HALF):
                strip = jnp.where((lane >= 16 * j) & (lane < 16 * j + 16), turn(own[base + j, :, cut], 16 * j - start), strip)
            packed[ew, n, 0:both, :] = strip
            rows = pl.ds(pl.multiple_of(base, 8), 8)
            packed[ew, n, both:both + 8, :] = jnp.where(
                lane8 < 16, turn(own_w[0, rows, cut], -start), turn(own_w[1, rows, cut], 16 - start))
        return 0

    def place_coef(e0, wl, wa, inside, chosen):
        kx = kxs[pl.ds(e0, 8), :]
        for t in chosen:
            cut = slice(128 * t, 128 * t + 128)
            l, a = wl[t] * (scale / 12.0), wa[t] * (scale / 12.0)
            planes = [-kx, l, 8.0 * a - DIFF_LAT * scale, -8.0 * a - DIFF_LAT * scale, a]
            for q, plane in enumerate(planes):
                if q == 0 and t != 1:
                    continue
                if inside is not None:
                    plane = plane * inside
                for j in range(8):
                    coef[e0 + j, q:q + 1, cut] = plane[j:j + 1, :]

    def centre(e):
        return (1.0 + 2.0 * DIFF_LAT) * scale - 2.0 * coef[e, 0:1, 128:256]

    def place_own(n, _):
        base = HALF * n
        rows = pl.ds(pl.multiple_of(base, 8), 8)
        wl, wa = ([None, turn(jnp.where(lane8 >= 64, own_w[q, rows, 0:128], own_w[q, rows, 128:256]), 64), None] for q in range(2))
        place_coef(pl.multiple_of(edge + base, 8), wl, wa, None, (1,))
        for j in range(HALF):
            r = base + j
            e = edge + r
            a, b = own[r, :, 0:128], own[r, :, 128:256]
            middle = centre(e)
            for t, piece in enumerate((turn(a, 16), turn(jnp.where(lane >= 64, a, b), 64), turn(b, 112))):
                cut = slice(128 * t, 128 * t + 128)
                even[0, e, :, cut] = piece[0:channels]
                diag[e, :, cut] = piece[channels:] * scale + middle
        return 0

    def place_lon(n, _):
        base = HALF * n
        rows = pl.ds(pl.multiple_of(base, 8), 8)
        w, e = near_lon[0, n, both:both + 8, :], near_lon[1, n, both:both + 8, :]
        wl, wa = ([jnp.where(lane8 < 16, turn(w, -16 * q), turn(own_w[q, rows, 0:128], 16)), None,
                   jnp.where(lane8 >= 112, turn(e, 112 - 16 * q), turn(own_w[q, rows, 128:256], 112))] for q in range(2))
        place_coef(pl.multiple_of(edge + base, 8), wl, wa, None, (0, 2))
        w, e = near_lon[0, n, 0:both, :], near_lon[1, n, 0:both, :]
        for j in range(HALF):
            r = edge + base + j
            middle = centre(r)
            for cut, keep, piece in ((slice(0, 128), lane < 16, turn(w, -16 * j)), (slice(256, 384), lane >= 112, turn(e, 112 - 16 * j))):
                even[0, r, :, cut] = jnp.where(keep[0:channels], piece[0:channels], even[0, r, :, cut])
                diag[r, :, cut] = jnp.where(keep[0:channels], piece[channels:] * scale + middle, diag[r, :, cut])
        return 0

    def place_halo(side, c):
        first = HALF * (1 - c) if side == 0 else HALF * c
        tile = tile_of(side, c)
        e0 = first if side == 0 else edge + lat + first
        inside = jnp.where(from_side(side), 1.0, 0.0).astype(f32)

        @pl.when(from_side(side))
        def _():
            for copy in lat_copies(side, c):
                copy.wait_recv()
            for ew in range(2):
                corner_copy(side, ew, c).wait_recv()

        def three(a, b, w, e, lanes, at):
            return (jnp.where(lanes < 16, turn(w, -at), turn(a, 16)), turn(jnp.where(lanes >= 64, a, b), 64),
                    jnp.where(lanes >= 112, turn(e, 112 - at), turn(b, 112)))

        west_strip, east_strip = near_corner.at[2 * side, tile], near_corner.at[2 * side + 1, tile]
        span = slice(first, first + 8)
        wl, wa = (three(near_lat_w[side, q, span, 0:128], near_lat_w[side, q, span, 128:256],
                        west_strip[both:both + 8, :], east_strip[both:both + 8, :], lane8, 16 * q) for q in range(2))
        place_coef(e0, wl, wa, inside, range(WINDOWS))
        for j in range(HALF):
            middle = centre(e0 + j)
            pieces = three(near_lat[side, first + j, :, 0:128], near_lat[side, first + j, :, 128:256],
                           west_strip[0:both, :], east_strip[0:both, :], lane, 16 * j)
            for t, piece in enumerate(pieces):
                cut = slice(128 * t, 128 * t + 128)
                even[0, e0 + j, :, cut] = piece[0:channels]
                diag[e0 + j, :, cut] = piece[channels:] * scale + middle

    def shift_of(k):
        theta = jnp.float32(THETA[0] * scale)
        for i in range(1, ITERS):
            theta = jnp.where(k == i, jnp.float32(THETA[i] * scale), theta)
        return theta

    def advance(src, dst, theta, starts):
        groups = [[e0 + GROUP * g + j for j in range(GROUP)] for e0 in starts for g in range(HALF // GROUP)]
        mixed, moved = [], []
        for picked in groups:
            stack = jnp.concatenate([src[e] for e in picked], axis=0)
            high = stack.astype(bf16)
            low = (stack - high.astype(f32)).astype(bf16)
            mixed.append(lax.dot_general(block[...], jnp.concatenate([high, low, high], axis=0), (((1,), (0,)), ((), ())),
                                         preferred_element_type=f32))
            sides = jnp.concatenate(
                [jnp.concatenate([high[:, 128 * t:128 * t + 128], low[:, 128 * t:128 * t + 128]], axis=1)
                 for t in range(WINDOWS)], axis=0)
            moved.append(lax.dot_general(sides, band[...], (((1,), (0,)), ((), ())), preferred_element_type=f32))
        for g, picked in enumerate(groups):
            for j, e in enumerate(picked):
                for t in range(WINDOWS):
                    cut = slice(128 * t, 128 * t + 128)
                    at = slice(size * t + channels * j, size * t + channels * (j + 1))

                    def weight(q):
                        return coef[e, q:q + 1, cut]

                    value = (diag[e, :, cut] - theta) * src[e, :, cut] + mixed[g][channels * j:channels * (j + 1), cut]
                    value = value + (coef[e, 0:1, 128:256] * moved[g][at, 0:128] + weight(1) * moved[g][at, 128:256])
                    value = value + weight(2) * src[e + 1, :, cut] + weight(3) * src[e - 1, :, cut]
                    dst[e, :, cut] = value + weight(4) * (src[e - 2, :, cut] - src[e + 2, :, cut])

    def two_levels(some):
        def run(n, _):
            some(2 * n, even.at[n], odd.at[n])
            some(2 * n + 1, odd.at[n], even.at[n + 1])
            return 0
        return run

    def interior(k, src, dst):
        theta = shift_of(k)

        def some(n, _):
            advance(src, dst, theta, (edge + 2 + 2 * k + HALF * n, edge + lat - 2 - HALF - 2 * k - HALF * n))
            return 0

        lax.fori_loop(0, jnp.where(k < 3, 2, 1), some, 0)

    def wedge(c):
        def some(k, src, dst):
            low = edge - HALF * (c + 1) + 2 + 2 * k
            advance(src, dst, shift_of(k), (low, rows_all - HALF - low))
        return some

    def dots(lo, hi, spans):
        pairs = [(k, i) for k, i in PAIRS if lo <= k <= hi]

        def one(t, _):
            cut = pl.ds(pl.multiple_of(t * 128, 128), 128)
            acc = (jnp.zeros((8, 128), f32),) * len(pairs)
            for start, stop in spans:
                def part(n, acc):
                    acc = list(acc)
                    for j in range(2):
                        e = start + 2 * n + j
                        for h in range(channels // 8):
                            x = [field(k)[e, 8 * h:8 * h + 8, cut] for k in range(hi + 1)]
                            for n_, (k, i) in enumerate(pairs):
                                acc[n_] = acc[n_] + x[k] * x[i]
                    return tuple(acc)

                acc = lax.fori_loop(0, (stop - start) // 2, part, acc)
            low = jnp.where(t == 1, 32, 16)
            kept = (lane8 >= low) & (lane8 < 128 - low)
            for n, (k, i) in enumerate(pairs):
                at = k * (k + 1) // 2 + i
                gram_acc[at] = gram_acc[at] + jnp.where(kept, acc[n], 0.0)
            return 0

        lax.fori_loop(0, WINDOWS, one, 0)

    for copy in winds:
        copy.wait()
    for q in range(2):
        half = own.at[:, pl.ds(q * channels, channels), :]
        pltpu.make_async_copy(half, half, load_sem.at[q]).wait()
    lax.fori_loop(0, tiles, pack, 0)
    pl.semaphore_wait(barrier, len(greeted))
    for c in range(2):
        for side in range(2):
            @pl.when(has(side))
            def _():
                copies = lat_copies(side, c)
                copies[0].start()
                for ew in range(2):
                    corner_copy(side, ew, c).start()
                for copy in copies[1:]:
                    copy.start()
        if c == 0:
            for ew in range(2):
                lon_copy(ew).start()
    for b in range(1, ny):
        greet(known, 0, b)
    lax.fori_loop(0, tiles, place_own, 0)
    for ew in range(2):
        lon_copy(ew).wait_recv()
    lax.fori_loop(0, tiles, place_lon, 0)
    lax.fori_loop(0, ITERS // 2, two_levels(interior), 0)
    ready = ITERS // 2
    for c in range(2):
        for side in range(2):
            place_halo(side, c)
        lax.fori_loop(0, ITERS // 2, two_levels(wedge(c)), 0)
        if c == 0:
            dots(0, ready, ((edge, edge + lat),))
            dots(ready + 1, ITERS, ((edge + HALF, edge + lat - HALF),))
    dots(ready + 1, ITERS, ((edge, edge + HALF), (edge + lat - HALF, edge + lat)))

    pl.semaphore_wait(known, ny - 1)
    sums = jnp.concatenate(
        [jnp.sum(gram_acc[n], axis=0, keepdims=True) for n in range(len(PAIRS))]
        + [jnp.zeros((128 - len(PAIRS), 128), f32)], axis=0)
    flat = lax.dot_general(jnp.ones((8, 128), f32), sums, (((1,), (1,)), ((), ())), precision=HI,
                           preferred_element_type=f32)
    mine[...] = flat[0:1, :]
    slots[total - 1] = flat[0:1, :]

    for n, (a, b) in enumerate(peers(nx, ny)):
        pltpu.make_async_remote_copy(
            src_ref=mine, dst_ref=slots.at[n], send_sem=red_sem.at[0], recv_sem=red_sem.at[1],
            device_id=(lax.rem(ix + a, nx), lax.rem(iy + b, ny)), device_id_type=MESH).start()
    arrived = slots.at[pl.ds(0, total - 1)]
    pltpu.make_async_copy(arrived, arrived, red_sem.at[1]).wait()
    pltpu.make_async_copy(arrived, arrived, red_sem.at[0]).wait()
    parts = [slots[n] for n in range(4)]
    for n in range(4, total):
        parts[n % 4] = parts[n % 4] + slots[n]
    whole = (parts[0] + parts[1]) + (parts[2] + parts[3])
    gram = [[None] * (ITERS + 1) for _ in range(ITERS + 1)]
    for n, (k, i) in enumerate(PAIRS):
        gram[k][i] = gram[i][k] = jnp.broadcast_to(whole[:, n:n + 1], (8, 128))
    answer, applied = small_solve(gram)
    for k in range(ITERS):
        splats[k] = answer[k]
    for k in range(ITERS + 1):
        splats[ITERS + k] = applied[k]

    def finish(n, _):
        for j in range(4):
            r = 4 * n + j
            for h in range(channels // 8):
                sub = slice(8 * h, 8 * h + 8)
                best, rest = [], []
                for t in range(WINDOWS):
                    cut = slice(128 * t, 128 * t + 128)
                    x = even[0, edge + r, sub, cut]
                    up = splats[0] * x
                    down = x - splats[ITERS] * x
                    for k in range(1, ITERS + 1):
                        x = field(k)[edge + r, sub, cut]
                        if k < ITERS:
                            up = up + splats[k] * x
                        down = down - splats[ITERS + k] * x
                    best.append(up)
                    rest.append(down)
                for q, (a, b, c) in enumerate((best, rest)):
                    b = turn(b, 64)
                    outs[q, r, sub, 0:128] = jnp.where(lane8 < 96, turn(a, 112), b)
                    outs[q, r, sub, 128:256] = jnp.where(lane8 < 32, b, turn(c, 16))
        return 0

    quarter = lat // 4
    for p in range(4):
        lax.fori_loop(quarter // 4 * p, quarter // 4 * (p + 1), finish, 0)
        for c in range(channels):
            for q, dst in enumerate((sol_hbm, res_hbm)):
                pltpu.make_async_copy(outs.at[q, pl.ds(quarter * p, quarter), c, :], dst.at[c, pl.ds(quarter * p, quarter), :],
                                      out_sem.at[q]).start()
    for ew in range(2):
        lon_copy(ew).wait_send()
    for side in range(2):
        @pl.when(has(side))
        def _():
            for c in range(2):
                for copy in lat_copies(side, c):
                    copy.wait_send()
                for ew in range(2):
                    corner_copy(side, ew, c).wait_send()
    for q, dst in enumerate((sol_hbm, res_hbm)):
        pltpu.make_async_copy(dst, dst, out_sem.at[q]).wait()


def solution(mesh):
    nx, ny = mesh.shape["gx"], mesh.shape["gy"]

    def per_device(forcing, damping, coupling, wind_lon, wind_lat):
        channels, lat, lon = forcing.shape
        f32 = jnp.float32
        vmem = pl.BlockSpec(memory_space=pltpu.VMEM)
        hbm = pl.BlockSpec(memory_space=pl.ANY)
        dma = pltpu.SemaphoreType.DMA
        shape = jax.ShapeDtypeStruct((channels, lat, lon), f32)
        rows_all, lanes = lat + 2 * HALO, 128 * WINDOWS
        packed = 2 * channels + 8
        return pl.pallas_call(
            functools.partial(kernel, nx, ny),
            out_shape=(shape, shape),
            in_specs=[hbm, hbm, vmem, hbm, hbm],
            out_specs=(hbm, hbm),
            scratch_shapes=[
                pltpu.VMEM((ITERS // 2 + 1, rows_all, channels, lanes), f32),
                pltpu.VMEM((ITERS // 2, rows_all, channels, lanes), f32),
                pltpu.VMEM((rows_all, channels, lanes), f32),
                pltpu.VMEM((rows_all, 8, lanes), f32),
                pltpu.VMEM((rows_all, 128), f32),
                pltpu.VMEM((GROUP * channels, 3 * GROUP * channels), jnp.bfloat16),
                pltpu.VMEM((256, 256), jnp.bfloat16),
                pltpu.VMEM((lat, 2 * channels, lon), f32),
                pltpu.VMEM((2, HALO, 2 * channels, lon), f32),
                pltpu.VMEM((2, lat, lon), f32),
                pltpu.VMEM((2, 2, HALO, lon), f32),
                pltpu.VMEM((2, lat // HALF, packed, 128), f32),
                pltpu.VMEM((2, lat // HALF, packed, 128), f32),
                pltpu.VMEM((4, 2, packed, 128), f32),
                pltpu.VMEM((len(PAIRS), 8, 128), f32),
                pltpu.VMEM((1, 128), f32),
                pltpu.VMEM((nx * ny, 1, 128), f32),
                pltpu.VMEM((2 * ITERS + 1, 8, 128), f32),
                pltpu.VMEM((2, lat, channels, lon), f32),
                dma((2,)), dma((2,)), dma((2,)),
                dma((2, 2, 3)), dma((2, 2, 3)), dma((2,)), dma((2,)), dma((4, 2)), dma((4, 2)), dma((2,)),
                pltpu.SemaphoreType.REGULAR,
            ],
            compiler_params=pltpu.CompilerParams(
                collective_id=0, has_side_effects=True, vmem_limit_bytes=63 * 1024 * 1024),
        )(forcing, damping, coupling, wind_lon, wind_lat)

    return jax.shard_map(
        per_device,
        mesh=mesh,
        in_specs=(P(None, "gy", "gx"), P(None, "gy", "gx"), P(), P("gy", "gx"), P("gy", "gx")),
        out_specs=(P(None, "gy", "gx"), P(None, "gy", "gx")),
        check_vma=False,
    )
```

time: 59.2 us -> 43.2 us (0.73)
  Pallas kernels: 55.7 us -> 39.5 us
    pallas_call x1, Pallas kernels: 55.7 us -> 39.5 us  [per_device(): pl.pallas_call(functools.partial(kernel, nx, ny), out_shape=(shape, shape...]
where the time goes in v1:
time: 43.2 us; the launch traced here: 42.9 us
  Pallas kernels  39.5 us (91%)
  local copies, waits for them, and re-layouts  2.74 us (6%)
  between operations  0.65 us (2%)
    pallas_call x1, Pallas kernels, per_device(): pl.pallas_call(functools.partial(kernel, nx, ny), out_shape=(shape, shape...  39.5 us
    unnamed x4, local copies, waits for them, and re-layouts  2.74 us

profile of v1, /device:TPU:1, one launch (start us, length us, event | category | flops | bytes accessed | tf_op | source)
XLA Modules:
  0.0 42.9 jit_solution(6932858501574264731)
XLA Ops:
  0.6 39.5 %shard_map.68 = (f32[16,32,256]{2,1,0:T(8,128)}, f32[16,32,256]{2,1,0:T(8,128)}) custom-call(f32[16,32,256]{2,1,0:T(8,128)} %f_hbm.1, f32[16,32,256]{2,1,0:T(8,128)} %d_hbm.1, f32[16,16]{1,0:T(8,128)} %c_ref.1, f32[32,256]{1,0:T(8,128)} %wl_hbm.1, f32[32,256]{1,0:T(8,128)} %wa_hbm.1), custom_call_target="tpu_custom_call" | custom-call | tf_op jit(solution)/shard_map/pallas_call | solution.py:534
  40.2 0.0 copy-start
  40.2 1.9 %copy.9 = f32[16,32,256]{2,1,0:T(8,128)} copy(f32[16,32,256]{2,1,0:T(8,128)} %get-tuple-element.4) | data formatting | bytes 1048576
  42.1 0.0 copy-done
  42.1 0.8 %copy.10 = f32[16,32,256]{2,1,0:T(8,128)} copy(f32[16,32,256]{2,1,0:T(8,128)S(1)} %copy-done) | data formatting | bytes 1048576
Async XLA Ops:
  40.2 2.0 %copy-start = (f32[16,32,256]{2,1,0:T(8,128)S(1)}, f32[16,32,256]{2,1,0:T(8,128)}, u32[]{:S(2)}) copy-start(f32[16,32,256]{2,1,0:T(8,128)} %get-tuple-element.5) | copy-start | bytes 1572868

commit v2 on v1

--- a/solution.py
+++ b/solution.py
@@ -108,10 +108,10 @@
     return sorted(offsets, key=lambda offset: (-hops(offset), offset))
 
 
-def kernel(nx, ny, f_hbm, d_hbm, c_ref, wl_hbm, wa_hbm, sol_hbm, res_hbm,
-           even, odd, diag, coef, kxs, block, band, own, near_lat, own_w, near_lat_w, packed, near_lon, near_corner,
-           gram_acc, mine, slots, splats, outs,
-           load_sem, wind_sem, out_sem, lat_send, lat_recv, lon_send, lon_recv, cor_send, cor_recv, red_sem, known):
+def kernel(nx, ny, f_hbm, d_hbm, c_ref, wl_hbm, wa_hbm, even, odd, splats,
+           diag, coef, kxs, block, band, own, near_lat, own_w, near_lat_w, packed, near_lon, near_corner,
+           gram_acc, mine, slots,
+           load_sem, wind_sem, lat_send, lat_recv, lon_send, lon_recv, cor_send, cor_recv, red_sem, known):
     channels, lat, lon = f_hbm.shape
     both = 2 * channels
     total = nx * ny
@@ -376,10 +376,10 @@
         lax.fori_loop(0, jnp.where(k < 3, 2, 1), some, 0)
 
     def wedge(c):
-        def some(k, src, dst):
+        for k in range(ITERS):
             low = edge - HALF * (c + 1) + 2 + 2 * k
-            advance(src, dst, shift_of(k), (low, rows_all - HALF - low))
-        return some
+            for e0 in (low, rows_all - HALF - low):
+                advance(field(k), field(k + 1), THETA[k] * scale, (e0,))
 
     def dots(lo, hi, spans):
         pairs = [(k, i) for k, i in PAIRS if lo <= k <= hi]
@@ -390,15 +390,15 @@
             for start, stop in spans:
                 def part(n, acc):
                     acc = list(acc)
-                    for j in range(2):
-                        e = start + 2 * n + j
+                    for j in range(4):
+                        e = start + 4 * n + j
                         for h in range(channels // 8):
                             x = [field(k)[e, 8 * h:8 * h + 8, cut] for k in range(hi + 1)]
                             for n_, (k, i) in enumerate(pairs):
                                 acc[n_] = acc[n_] + x[k] * x[i]
                     return tuple(acc)
 
-                acc = lax.fori_loop(0, (stop - start) // 2, part, acc)
+                acc = lax.fori_loop(0, (stop - start) // 4, part, acc)
             low = jnp.where(t == 1, 32, 16)
             kept = (lane8 >= low) & (lane8 < 128 - low)
             for n, (k, i) in enumerate(pairs):
@@ -436,12 +436,13 @@
     lax.fori_loop(0, tiles, place_lon, 0)
     lax.fori_loop(0, ITERS // 2, two_levels(interior), 0)
     ready = ITERS // 2
+    dots(0, ready, ((edge + HALF, edge + lat - HALF),))
     for c in range(2):
         for side in range(2):
             place_halo(side, c)
-        lax.fori_loop(0, ITERS // 2, two_levels(wedge(c)), 0)
+        wedge(c)
         if c == 0:
-            dots(0, ready, ((edge, edge + lat),))
+            dots(0, ready, ((edge, edge + HALF), (edge + lat - HALF, edge + lat)))
             dots(ready + 1, ITERS, ((edge + HALF, edge + lat - HALF),))
     dots(ready + 1, ITERS, ((edge, edge + HALF), (edge + lat - HALF, edge + lat)))
 
@@ -474,37 +475,6 @@
     for k in range(ITERS + 1):
         splats[ITERS + k] = applied[k]
 
-    def finish(n, _):
-        for j in range(4):
-            r = 4 * n + j
-            for h in range(channels // 8):
-                sub = slice(8 * h, 8 * h + 8)
-                best, rest = [], []
-                for t in range(WINDOWS):
-                    cut = slice(128 * t, 128 * t + 128)
-                    x = even[0, edge + r, sub, cut]
-                    up = splats[0] * x
-                    down = x - splats[ITERS] * x
-                    for k in range(1, ITERS + 1):
-                        x = field(k)[edge + r, sub, cut]
-                        if k < ITERS:
-                            up = up + splats[k] * x
-                        down = down - splats[ITERS + k] * x
-                    best.append(up)
-                    rest.append(down)
-                for q, (a, b, c) in enumerate((best, rest)):
-                    b = turn(b, 64)
-                    outs[q, r, sub, 0:128] = jnp.where(lane8 < 96, turn(a, 112), b)
-                    outs[q, r, sub, 128:256] = jnp.where(lane8 < 32, b, turn(c, 16))
-        return 0
-
-    quarter = lat // 4
-    for p in range(4):
-        lax.fori_loop(quarter // 4 * p, quarter // 4 * (p + 1), finish, 0)
-        for c in range(channels):
-            for q, dst in enumerate((sol_hbm, res_hbm)):
-                pltpu.make_async_copy(outs.at[q, pl.ds(quarter * p, quarter), c, :], dst.at[c, pl.ds(quarter * p, quarter), :],
-                                      out_sem.at[q]).start()
     for ew in range(2):
         lon_copy(ew).wait_send()
     for side in range(2):
@@ -515,6 +485,37 @@
                     copy.wait_send()
                 for ew in range(2):
                     corner_copy(side, ew, c).wait_send()
+
+
+def finish(even, odd, splats, sol_hbm, res_hbm, outs, out_sem):
+    channels, lat, _ = sol_hbm.shape
+    lane = lax.broadcasted_iota(jnp.int32, (8, 128), 1)
+    quarter = lat // 4
+    for r in range(lat):
+        for h in range(channels // 8):
+            sub = slice(8 * h, 8 * h + 8)
+            best, rest = [], []
+            for t in range(WINDOWS):
+                cut = slice(128 * t, 128 * t + 128)
+                x = even[0, HALO + r, sub, cut]
+                up = splats[0] * x
+                down = x - splats[ITERS] * x
+                for k in range(1, ITERS + 1):
+                    x = (odd if k % 2 else even)[k // 2, HALO + r, sub, cut]
+                    if k < ITERS:
+                        up = up + splats[k] * x
+                    down = down - splats[ITERS + k] * x
+                best.append(up)
+                rest.append(down)
+            for q, (a, b, c) in enumerate((best, rest)):
+                b = pltpu.roll(b, 64, 1)
+                outs[q, r, sub, 0:128] = jnp.where(lane < 96, pltpu.roll(a, 112, 1), b)
+                outs[q, r, sub, 128:256] = jnp.where(lane < 32, b, pltpu.roll(c, 16, 1))
+        if (r + 1) % quarter == 0:
+            rows = pl.ds(r + 1 - quarter, quarter)
+            for c in range(channels):
+                for q, dst in enumerate((sol_hbm, res_hbm)):
+                    pltpu.make_async_copy(outs.at[q, rows, c, :], dst.at[c, rows, :], out_sem.at[q]).start()
     for q, dst in enumerate((sol_hbm, res_hbm)):
         pltpu.make_async_copy(dst, dst, out_sem.at[q]).wait()
 
@@ -526,19 +527,21 @@
         channels, lat, lon = forcing.shape
         f32 = jnp.float32
         vmem = pl.BlockSpec(memory_space=pltpu.VMEM)
-        hbm = pl.BlockSpec(memory_space=pl.ANY)
+        hbm = pl.BlockSpec(memory_space=pltpu.HBM)
         dma = pltpu.SemaphoreType.DMA
         shape = jax.ShapeDtypeStruct((channels, lat, lon), f32)
         rows_all, lanes = lat + 2 * HALO, 128 * WINDOWS
         packed = 2 * channels + 8
-        return pl.pallas_call(
+        even, odd, splats = pl.pallas_call(
             functools.partial(kernel, nx, ny),
-            out_shape=(shape, shape),
-            in_specs=[hbm, hbm, vmem, hbm, hbm],
-            out_specs=(hbm, hbm),
-            scratch_shapes=[
+            out_shape=(
                 pltpu.VMEM((ITERS // 2 + 1, rows_all, channels, lanes), f32),
                 pltpu.VMEM((ITERS // 2, rows_all, channels, lanes), f32),
+                pltpu.VMEM((2 * ITERS + 1, 8, 128), f32),
+            ),
+            in_specs=[hbm, hbm, vmem, hbm, hbm],
+            out_specs=(vmem, vmem, vmem),
+            scratch_shapes=[
                 pltpu.VMEM((rows_all, channels, lanes), f32),
                 pltpu.VMEM((rows_all, 8, lanes), f32),
                 pltpu.VMEM((rows_all, 128), f32),
@@ -554,15 +557,21 @@
                 pltpu.VMEM((len(PAIRS), 8, 128), f32),
                 pltpu.VMEM((1, 128), f32),
                 pltpu.VMEM((nx * ny, 1, 128), f32),
-                pltpu.VMEM((2 * ITERS + 1, 8, 128), f32),
-                pltpu.VMEM((2, lat, channels, lon), f32),
-                dma((2,)), dma((2,)), dma((2,)),
+                dma((2,)), dma((2,)),
                 dma((2, 2, 3)), dma((2, 2, 3)), dma((2,)), dma((2,)), dma((4, 2)), dma((4, 2)), dma((2,)),
                 pltpu.SemaphoreType.REGULAR,
             ],
             compiler_params=pltpu.CompilerParams(
-                collective_id=0, has_side_effects=True, vmem_limit_bytes=63 * 1024 * 1024),
+                collective_id=0, has_side_effects=True, vmem_limit_bytes=52_800_000),
         )(forcing, damping, coupling, wind_lon, wind_lat)
+        return pl.pallas_call(
+            finish,
+            out_shape=(shape, shape),
+            in_specs=[vmem, vmem, vmem],
+            out_specs=(hbm, hbm),
+            scratch_shapes=[pltpu.VMEM((2, lat, channels, lon), f32), dma((2,))],
+            compiler_params=pltpu.CompilerParams(vmem_limit_bytes=16 * 1024 * 1024),
+        )(even, odd, splats)
 
     return jax.shard_map(
         per_device,

time: 43.2 us -> 39.2 us (0.907)
  local copies, waits for them, and re-layouts: 2.74 us -> 0 us
  Pallas kernels: 39.5 us -> 38.3 us
    unnamed x4 -> x0, local copies, waits for them, and re-layouts: 2.74 us -> none
    pallas_call x1 -> x2, Pallas kernels: 39.5 us -> 38.3 us  [the longest x1 35.9 us: per_device(): pl.pallas_call(functools.partial(kernel, nx, ny), out_shape=(pltpu.VMEM((...]
where the time goes in v2:
time: 39.2 us; the launch traced here: 38.9 us
  Pallas kernels  38.3 us (98%)
  between operations  0.64 us (2%)
    pallas_call x1, Pallas kernels, per_device(): pl.pallas_call(functools.partial(kernel, nx, ny), out_shape=(pltpu.VMEM((...  35.9 us
    pallas_call x1, Pallas kernels, per_device(): pl.pallas_call(finish, out_shape=(shape, shape), in_specs=[vmem, vmem, vm...  2.34 us

profile of v2, /device:TPU:1, one launch (start us, length us, event | category | flops | bytes accessed | tf_op | source)
XLA Modules:
  0.0 38.9 jit_solution(12813143621209664209)
XLA Ops:
  0.6 35.9 %shard_map.68 = (f32[5,64,16,384]{3,2,1,0:T(8,128)S(1)}, f32[4,64,16,384]{3,2,1,0:T(8,128)S(1)}, f32[17,8,128]{2,1,0:T(8,128)S(1)}) custom-call(f32[16,32,256]{2,1,0:T(8,128)} %f_hbm.1, f32[16,32,256]{2,1,0:T(8,128)} %d_hbm.1, f32[16,16]{1,0:T(8,128)} %c_ref.1, f32[32,256]{1,0:T(8,128)} %wl_hbm.1, f32[32,256]{1,0:T(8,128)} %wa_hbm.1), custom_call_target="tpu_custom_call" | custom-call | tf_op jit(solution)/shard_map/pallas_call | solution.py:535
  36.6 2.3 %shard_map.69 = (f32[16,32,256]{2,1,0:T(8,128)}, f32[16,32,256]{2,1,0:T(8,128)}) custom-call(f32[5,64,16,384]{3,2,1,0:T(8,128)S(1)} %get-tuple-element.5.even, f32[4,64,16,384]{3,2,1,0:T(8,128)S(1)} %get-tuple-element.6.odd, f32[17,8,128]{2,1,0:T(8,128)S(1)} %get-tuple-element.7.splats), custom_call_target="tpu_custom_call" | custom-call | tf_op jit(solution)/shard_map/pallas_call | solution.py:567

commit v3 on v2

--- a/solution.py
+++ b/solution.py
@@ -132,10 +132,22 @@
     def greet(sem, a, b):
         pl.semaphore_signal(sem, inc=1, device_id=(lax.rem(ix + a, nx), lax.rem(iy + b, ny)), device_id_type=MESH)
 
-    greeted = [(1, 1), (1, ny - 1), (nx - 1, 1), (nx - 1, ny - 1), (0, 1), (0, ny - 1), (1, 0), (nx - 1, 0)]
-    greeted += [(a, 0) for a in range(2, nx - 1)] + [(0, b) for b in range(2, ny - 1)]
-    for a, b in greeted:
+    close = [(0, 1), (0, ny - 1), (1, 0), (nx - 1, 0)]
+    rounds = [
+        close,
+        close + [(0, 2), (0, ny - 2), (2, 0), (nx - 2, 0)],
+        [(0, b) for b in range(1, 5)] + [(0, ny - b) for b in range(1, 5)],
+        [(a, 0) for a in range(1, nx)],
+    ]
+    for a, b in close:
         greet(barrier, a, b)
+
+    def tell(n):
+        for a, b in rounds[n]:
+            greet(known.at[n], a, b)
+
+    def hear(n):
+        pl.semaphore_wait(known.at[n], len(rounds[n]))
 
     winds = [pltpu.make_async_copy(wl_hbm, own_w.at[0], wind_sem.at[0]), pltpu.make_async_copy(wa_hbm, own_w.at[1], wind_sem.at[1])]
     for copy in winds:
@@ -408,32 +420,66 @@
 
         lax.fori_loop(0, WINDOWS, one, 0)
 
+    def rim_dots(first, last):
+        for t in range(WINDOWS):
+            cut = slice(128 * t, 128 * t + 128)
+            acc = {}
+            for p in range(HALF // 2):
+                for e in (edge + 2 * p, edge + 2 * p + 1, edge + lat - 1 - 2 * p, edge + lat - 2 - 2 * p):
+                    for h in range(channels // 8):
+                        levels = range(first(p), last(p) + 1)
+                        if not len(levels):
+                            continue
+                        x = [field(k)[e, 8 * h:8 * h + 8, cut] for k in range(last(p) + 1)]
+                        for k in levels:
+                            for i in range(k + 1):
+                                term = x[k] * x[i]
+                                acc[k, i] = acc[k, i] + term if (k, i) in acc else term
+            low = 32 if t == 1 else 16
+            kept = (lane8 >= low) & (lane8 < 128 - low)
+            for (k, i), value in acc.items():
+                at = k * (k + 1) // 2 + i
+                gram_acc[at] = gram_acc[at] + jnp.where(kept, value, 0.0)
+
     for copy in winds:
         copy.wait()
     for q in range(2):
         half = own.at[:, pl.ds(q * channels, channels), :]
         pltpu.make_async_copy(half, half, load_sem.at[q]).wait()
-    lax.fori_loop(0, tiles, pack, 0)
-    pl.semaphore_wait(barrier, len(greeted))
-    for c in range(2):
+    pl.semaphore_wait(barrier, len(close))
+    tell(0)
+
+    def send_lat(c):
         for side in range(2):
             @pl.when(has(side))
             def _():
-                copies = lat_copies(side, c)
-                copies[0].start()
+                for copy in lat_copies(side, c):
+                    copy.start()
+
+    def send_corners(c):
+        for side in range(2):
+            @pl.when(has(side))
+            def _():
                 for ew in range(2):
                     corner_copy(side, ew, c).start()
-                for copy in copies[1:]:
-                    copy.start()
-        if c == 0:
-            for ew in range(2):
-                lon_copy(ew).start()
-    for b in range(1, ny):
-        greet(known, 0, b)
+
+    send_lat(0)
+    lax.fori_loop(0, tiles, pack, 0)
+    for ew in range(2):
+        lon_copy(ew).start()
+    hear(0)
+    tell(1)
+    send_corners(0)
+    send_lat(1)
+    send_corners(1)
     lax.fori_loop(0, tiles, place_own, 0)
+    hear(1)
+    tell(2)
     for ew in range(2):
         lon_copy(ew).wait_recv()
     lax.fori_loop(0, tiles, place_lon, 0)
+    hear(2)
+    tell(3)
     lax.fori_loop(0, ITERS // 2, two_levels(interior), 0)
     ready = ITERS // 2
     dots(0, ready, ((edge + HALF, edge + lat - HALF),))
@@ -444,9 +490,10 @@
         if c == 0:
             dots(0, ready, ((edge, edge + HALF), (edge + lat - HALF, edge + lat)))
             dots(ready + 1, ITERS, ((edge + HALF, edge + lat - HALF),))
-    dots(ready + 1, ITERS, ((edge, edge + HALF), (edge + lat - HALF, edge + lat)))
-
-    pl.semaphore_wait(known, ny - 1)
+            rim_dots(lambda p: ready + 1, lambda p: ready + p)
+    rim_dots(lambda p: ready + 1 + p, lambda p: ITERS)
+
+    hear(3)
     sums = jnp.concatenate(
         [jnp.sum(gram_acc[n], axis=0, keepdims=True) for n in range(len(PAIRS))]
         + [jnp.zeros((128 - len(PAIRS), 128), f32)], axis=0)
@@ -509,13 +556,15 @@
                 rest.append(down)
             for q, (a, b, c) in enumerate((best, rest)):
                 b = pltpu.roll(b, 64, 1)
-                outs[q, r, sub, 0:128] = jnp.where(lane < 96, pltpu.roll(a, 112, 1), b)
-                outs[q, r, sub, 128:256] = jnp.where(lane < 32, b, pltpu.roll(c, 16, 1))
+                spread = pl.ds(8 * h * lat + r, 8, stride=lat)
+                outs[q, 0, spread, :] = jnp.where(lane < 96, pltpu.roll(a, 112, 1), b)
+                outs[q, 1, spread, :] = jnp.where(lane < 32, b, pltpu.roll(c, 16, 1))
         if (r + 1) % quarter == 0:
             rows = pl.ds(r + 1 - quarter, quarter)
-            for c in range(channels):
-                for q, dst in enumerate((sol_hbm, res_hbm)):
-                    pltpu.make_async_copy(outs.at[q, rows, c, :], dst.at[c, rows, :], out_sem.at[q]).start()
+            for q, dst in enumerate((sol_hbm, res_hbm)):
+                for t in range(2):
+                    src = outs.at[q, t].reshape(channels, lat, 128)
+                    pltpu.make_async_copy(src.at[:, rows, :], dst.at[:, rows, pl.ds(128 * t, 128)], out_sem.at[q]).start()
     for q, dst in enumerate((sol_hbm, res_hbm)):
         pltpu.make_async_copy(dst, dst, out_sem.at[q]).wait()
 
@@ -559,7 +608,7 @@
                 pltpu.VMEM((nx * ny, 1, 128), f32),
                 dma((2,)), dma((2,)),
                 dma((2, 2, 3)), dma((2, 2, 3)), dma((2,)), dma((2,)), dma((4, 2)), dma((4, 2)), dma((2,)),
-                pltpu.SemaphoreType.REGULAR,
+                pltpu.SemaphoreType.REGULAR((4,)),
             ],
             compiler_params=pltpu.CompilerParams(
                 collective_id=0, has_side_effects=True, vmem_limit_bytes=52_800_000),
@@ -569,7 +618,7 @@
             out_shape=(shape, shape),
             in_specs=[vmem, vmem, vmem],
             out_specs=(hbm, hbm),
-            scratch_shapes=[pltpu.VMEM((2, lat, channels, lon), f32), dma((2,))],
+            scratch_shapes=[pltpu.VMEM((2, 2, channels * lat, 128), f32), dma((2,))],
             compiler_params=pltpu.CompilerParams(vmem_limit_bytes=16 * 1024 * 1024),
         )(even, odd, splats)
 

time: 39.2 us -> 41.3 us (1.054)
  Pallas kernels: 38.3 us -> 40.4 us
    pallas_call x1, Pallas kernels: 35.9 us -> 38.3 us  [per_device(): pl.pallas_call(functools.partial(kernel, nx, ny), out_shape=(pltpu.VMEM((...]
where the time goes in v3:
time: 41.3 us; the launch traced here: 41.1 us
  Pallas kernels  40.4 us (98%)
  between operations  0.64 us (2%)
    pallas_call x1, Pallas kernels, per_device(): pl.pallas_call(functools.partial(kernel, nx, ny), out_shape=(pltpu.VMEM((...  38.3 us
    pallas_call x1, Pallas kernels, per_device(): pl.pallas_call(finish, out_shape=(shape, shape), in_specs=[vmem, vmem, vm...  2.16 us

profile of v3, /device:TPU:1, one launch (start us, length us, event | category | flops | bytes accessed | tf_op | source)
XLA Modules:
  0.0 41.1 jit_solution(3564564161879356948)
XLA Ops:
  0.6 38.3 %shard_map.68 = (f32[5,64,16,384]{3,2,1,0:T(8,128)S(1)}, f32[4,64,16,384]{3,2,1,0:T(8,128)S(1)}, f32[17,8,128]{2,1,0:T(8,128)S(1)}) custom-call(f32[16,32,256]{2,1,0:T(8,128)} %f_hbm.1, f32[16,32,256]{2,1,0:T(8,128)} %d_hbm.1, f32[16,16]{1,0:T(8,128)} %c_ref.1, f32[32,256]{1,0:T(8,128)} %wl_hbm.1, f32[32,256]{1,0:T(8,128)} %wa_hbm.1), custom_call_target="tpu_custom_call" | custom-call | tf_op jit(solution)/shard_map/pallas_call | solution.py:584
  38.9 2.2 %shard_map.69 = (f32[16,32,256]{2,1,0:T(8,128)}, f32[16,32,256]{2,1,0:T(8,128)}) custom-call(f32[5,64,16,384]{3,2,1,0:T(8,128)S(1)} %get-tuple-element.5.even, f32[4,64,16,384]{3,2,1,0:T(8,128)S(1)} %get-tuple-element.6.odd, f32[17,8,128]{2,1,0:T(8,128)S(1)} %get-tuple-element.7.splats), custom_call_target="tpu_custom_call" | custom-call | tf_op jit(solution)/shard_map/pallas_call | solution.py:616

commit v4 on v3

--- a/solution.py
+++ b/solution.py
@@ -111,7 +111,7 @@
 def kernel(nx, ny, f_hbm, d_hbm, c_ref, wl_hbm, wa_hbm, even, odd, splats,
            diag, coef, kxs, block, band, own, near_lat, own_w, near_lat_w, packed, near_lon, near_corner,
            gram_acc, mine, slots,
-           load_sem, wind_sem, lat_send, lat_recv, lon_send, lon_recv, cor_send, cor_recv, red_sem, known):
+           load_sem, lat_send, lat_recv, lon_send, lon_recv, red_sem, known):
     channels, lat, lon = f_hbm.shape
     both = 2 * channels
     total = nx * ny
@@ -149,12 +149,12 @@
     def hear(n):
         pl.semaphore_wait(known.at[n], len(rounds[n]))
 
-    winds = [pltpu.make_async_copy(wl_hbm, own_w.at[0], wind_sem.at[0]), pltpu.make_async_copy(wa_hbm, own_w.at[1], wind_sem.at[1])]
+    winds = [pltpu.make_async_copy(wl_hbm, own_w.at[0], load_sem.at[1]), pltpu.make_async_copy(wa_hbm, own_w.at[1], load_sem.at[1])]
     for copy in winds:
         copy.start()
     for c in range(channels):
         for q, src in enumerate((f_hbm, d_hbm)):
-            pltpu.make_async_copy(src.at[c], own.at[:, q * channels + c, :], load_sem.at[q]).start()
+            pltpu.make_async_copy(src.at[c], own.at[:, q * channels + c, :], load_sem.at[0]).start()
 
     def spread(n):
         row = lax.broadcasted_iota(jnp.int32, (n, channels), 0)
@@ -210,10 +210,10 @@
             out.append(pltpu.make_async_remote_copy(
                 src_ref=own.at[pl.ds(base + start, count), pl.ds(sub, subs), :],
                 dst_ref=near_lat.at[side, pl.ds(start, count), pl.ds(sub, subs), :],
-                send_sem=lat_send.at[side, c, n], recv_sem=lat_recv.at[side, c, n], device_id=to, device_id_type=MESH))
+                send_sem=lat_send.at[side], recv_sem=lat_recv.at[side, c], device_id=to, device_id_type=MESH))
         out.append(pltpu.make_async_remote_copy(
             src_ref=own_w.at[:, pl.ds(base + first, HALF), :], dst_ref=near_lat_w.at[side, :, pl.ds(first, HALF), :],
-            send_sem=lat_send.at[side, c, 2], recv_sem=lat_recv.at[side, c, 2], device_id=to, device_id_type=MESH))
+            send_sem=lat_send.at[side], recv_sem=lat_recv.at[side, c], device_id=to, device_id_type=MESH))
         return out
 
     def tile_of(side, c):
@@ -223,7 +223,7 @@
         slot, tile = 2 * side + ew, tile_of(side, c)
         return pltpu.make_async_remote_copy(
             src_ref=packed.at[ew, tile + (tiles - 2 if side == 0 else 0)], dst_ref=near_corner.at[slot, tile],
-            send_sem=cor_send.at[slot, c], recv_sem=cor_recv.at[slot, c],
+            send_sem=lat_send.at[side], recv_sem=lat_recv.at[side, c],
             device_id=(east if ew == 0 else west, iy + 1 if side == 0 else iy - 1), device_id_type=MESH)
 
     def lon_copy(ew):
@@ -315,10 +315,8 @@
 
         @pl.when(from_side(side))
         def _():
-            for copy in lat_copies(side, c):
-                copy.wait_recv()
-            for ew in range(2):
-                corner_copy(side, ew, c).wait_recv()
+            whole = diag.at[pl.ds(0, 13)] if c == 0 else coef.at[pl.ds(0, 35), :, pl.ds(0, 256)]
+            pltpu.make_async_copy(whole, whole, lat_recv.at[side, c]).wait()
 
         def three(a, b, w, e, lanes, at):
             return (jnp.where(lanes < 16, turn(w, -at), turn(a, 16)), turn(jnp.where(lanes >= 64, a, b), 64),
@@ -441,11 +439,8 @@
                 at = k * (k + 1) // 2 + i
                 gram_acc[at] = gram_acc[at] + jnp.where(kept, value, 0.0)
 
-    for copy in winds:
-        copy.wait()
-    for q in range(2):
-        half = own.at[:, pl.ds(q * channels, channels), :]
-        pltpu.make_async_copy(half, half, load_sem.at[q]).wait()
+    pltpu.make_async_copy(own_w, own_w, load_sem.at[1]).wait()
+    pltpu.make_async_copy(own, own, load_sem.at[0]).wait()
     pl.semaphore_wait(barrier, len(close))
     tell(0)
 
@@ -473,14 +468,12 @@
     send_lat(1)
     send_corners(1)
     lax.fori_loop(0, tiles, place_own, 0)
-    hear(1)
-    tell(2)
     for ew in range(2):
         lon_copy(ew).wait_recv()
     lax.fori_loop(0, tiles, place_lon, 0)
-    hear(2)
-    tell(3)
     lax.fori_loop(0, ITERS // 2, two_levels(interior), 0)
+    hear(1)
+    tell(2)
     ready = ITERS // 2
     dots(0, ready, ((edge + HALF, edge + lat - HALF),))
     for c in range(2):
@@ -488,6 +481,8 @@
             place_halo(side, c)
         wedge(c)
         if c == 0:
+            hear(2)
+            tell(3)
             dots(0, ready, ((edge, edge + HALF), (edge + lat - HALF, edge + lat)))
             dots(ready + 1, ITERS, ((edge + HALF, edge + lat - HALF),))
             rim_dots(lambda p: ready + 1, lambda p: ready + p)
@@ -527,11 +522,8 @@
     for side in range(2):
         @pl.when(has(side))
         def _():
-            for c in range(2):
-                for copy in lat_copies(side, c):
-                    copy.wait_send()
-                for ew in range(2):
-                    corner_copy(side, ew, c).wait_send()
+            whole = even.at[0, pl.ds(0, 37), :, pl.ds(0, 256)]
+            pltpu.make_async_copy(whole, whole, lat_send.at[side]).wait()
 
 
 def finish(even, odd, splats, sol_hbm, res_hbm, outs, out_sem):
@@ -606,8 +598,8 @@
                 pltpu.VMEM((len(PAIRS), 8, 128), f32),
                 pltpu.VMEM((1, 128), f32),
                 pltpu.VMEM((nx * ny, 1, 128), f32),
-                dma((2,)), dma((2,)),
-                dma((2, 2, 3)), dma((2, 2, 3)), dma((2,)), dma((2,)), dma((4, 2)), dma((4, 2)), dma((2,)),
+                dma((2,)),
+                dma((2,)), dma((2, 2)), dma((2,)), dma((2,)), dma((2,)),
                 pltpu.SemaphoreType.REGULAR((4,)),
             ],
             compiler_params=pltpu.CompilerParams(

time: 41.3 us -> 36.8 us (0.89)
  Pallas kernels: 40.4 us -> 35.9 us
    pallas_call x1, Pallas kernels: 38.3 us -> 33.8 us  [per_device(): pl.pallas_call(functools.partial(kernel, nx, ny), out_shape=(pltpu.VMEM((...]
where the time goes in v4:
time: 36.8 us; the launch traced here: 36.6 us
  Pallas kernels  35.9 us (98%)
  between operations  0.64 us (2%)
    pallas_call x1, Pallas kernels, per_device(): pl.pallas_call(functools.partial(kernel, nx, ny), out_shape=(pltpu.VMEM((...  33.8 us
    pallas_call x1, Pallas kernels, per_device(): pl.pallas_call(finish, out_shape=(shape, shape), in_specs=[vmem, vmem, vm...  2.16 us

profile of v4, /device:TPU:1, one launch (start us, length us, event | category | flops | bytes accessed | tf_op | source)
XLA Modules:
  0.0 36.6 jit_solution(17743662155705147905)
XLA Ops:
  0.6 33.8 %shard_map.68 = (f32[5,64,16,384]{3,2,1,0:T(8,128)S(1)}, f32[4,64,16,384]{3,2,1,0:T(8,128)S(1)}, f32[17,8,128]{2,1,0:T(8,128)S(1)}) custom-call(f32[16,32,256]{2,1,0:T(8,128)} %f_hbm.1, f32[16,32,256]{2,1,0:T(8,128)} %d_hbm.1, f32[16,16]{1,0:T(8,128)} %c_ref.1, f32[32,256]{1,0:T(8,128)} %wl_hbm.1, f32[32,256]{1,0:T(8,128)} %wa_hbm.1), custom_call_target="tpu_custom_call" | custom-call | tf_op jit(solution)/shard_map/pallas_call | solution.py:576
  34.4 2.2 %shard_map.69 = (f32[16,32,256]{2,1,0:T(8,128)}, f32[16,32,256]{2,1,0:T(8,128)}) custom-call(f32[5,64,16,384]{3,2,1,0:T(8,128)S(1)} %get-tuple-element.5.even, f32[4,64,16,384]{3,2,1,0:T(8,128)S(1)} %get-tuple-element.6.odd, f32[17,8,128]{2,1,0:T(8,128)S(1)} %get-tuple-element.7.splats), custom_call_target="tpu_custom_call" | custom-call | tf_op jit(solution)/shard_map/pallas_call | solution.py:608

commit v5 on v4

--- a/solution.py
+++ b/solution.py
@@ -130,15 +130,27 @@
     barrier = pltpu.get_barrier_semaphore()
 
     def greet(sem, a, b):
-        pl.semaphore_signal(sem, inc=1, device_id=(lax.rem(ix + a, nx), lax.rem(iy + b, ny)), device_id_type=MESH)
-
-    close = [(0, 1), (0, ny - 1), (1, 0), (nx - 1, 0)]
-    rounds = [
-        close,
-        close + [(0, 2), (0, ny - 2), (2, 0), (nx - 2, 0)],
-        [(0, b) for b in range(1, 5)] + [(0, ny - b) for b in range(1, 5)],
-        [(a, 0) for a in range(1, nx)],
-    ]
+        def signal():
+            pl.semaphore_signal(sem, inc=1, device_id=(lax.rem(ix + a, nx), iy + b), device_id_type=MESH)
+
+        if b == 0:
+            signal()
+        else:
+            pl.when(iy + b < ny if b > 0 else iy + b >= 0)(signal)
+
+    def line(n):
+        return [(0, b) for b in range(1, n + 1)] + [(0, -b) for b in range(1, n + 1)]
+
+    def ring(n):
+        return [(a, 0) for a in range(1, n + 1)] + [(nx - a, 0) for a in range(1, n + 1)]
+
+    def answers(offsets):
+        fixed = sum(1 for _, b in offsets if b == 0)
+        reach = max(b for _, b in offsets)
+        return fixed + jnp.minimum(ny - 1 - iy, reach) + jnp.minimum(iy, reach)
+
+    close = line(1) + ring(1)
+    rounds = [line(1), ring(1), line(2) + ring(2), line(4), line(8), [(a, 0) for a in range(1, nx)]]
     for a, b in close:
         greet(barrier, a, b)
 
@@ -147,7 +159,7 @@
             greet(known.at[n], a, b)
 
     def hear(n):
-        pl.semaphore_wait(known.at[n], len(rounds[n]))
+        pl.semaphore_wait(known.at[n], answers(rounds[n]))
 
     winds = [pltpu.make_async_copy(wl_hbm, own_w.at[0], load_sem.at[1]), pltpu.make_async_copy(wa_hbm, own_w.at[1], load_sem.at[1])]
     for copy in winds:
@@ -336,14 +348,9 @@
                 even[0, e0 + j, :, cut] = piece[0:channels]
                 diag[e0 + j, :, cut] = piece[channels:] * scale + middle
 
-    def shift_of(k):
-        theta = jnp.float32(THETA[0] * scale)
-        for i in range(1, ITERS):
-            theta = jnp.where(k == i, jnp.float32(THETA[i] * scale), theta)
-        return theta
-
-    def advance(src, dst, theta, starts):
-        groups = [[e0 + GROUP * g + j for j in range(GROUP)] for e0 in starts for g in range(HALF // GROUP)]
+    def advance(level, start, count):
+        src, dst, theta = field(level), field(level + 1), THETA[level] * scale
+        groups = [[start + GROUP * g + j for j in range(GROUP)] for g in range(count)]
         mixed, moved = [], []
         for picked in groups:
             stack = jnp.concatenate([src[e] for e in picked], axis=0)
@@ -369,27 +376,17 @@
                     value = value + weight(2) * src[e + 1, :, cut] + weight(3) * src[e - 1, :, cut]
                     dst[e, :, cut] = value + weight(4) * (src[e - 2, :, cut] - src[e + 2, :, cut])
 
-    def two_levels(some):
-        def run(n, _):
-            some(2 * n, even.at[n], odd.at[n])
-            some(2 * n + 1, odd.at[n], even.at[n + 1])
-            return 0
-        return run
-
-    def interior(k, src, dst):
-        theta = shift_of(k)
-
-        def some(n, _):
-            advance(src, dst, theta, (edge + 2 + 2 * k + HALF * n, edge + lat - 2 - HALF - 2 * k - HALF * n))
-            return 0
-
-        lax.fori_loop(0, jnp.where(k < 3, 2, 1), some, 0)
+    def interior():
+        for k in range(ITERS - 1):
+            count = (lat - 4 - 4 * k) // GROUP
+            for g in range(0, count, 2):
+                advance(k, edge + 2 + 2 * k + GROUP * g, min(2, count - g))
 
     def wedge(c):
         for k in range(ITERS):
             low = edge - HALF * (c + 1) + 2 + 2 * k
             for e0 in (low, rows_all - HALF - low):
-                advance(field(k), field(k + 1), THETA[k] * scale, (e0,))
+                advance(k, e0, HALF // GROUP)
 
     def dots(lo, hi, spans):
         pairs = [(k, i) for k, i in PAIRS if lo <= k <= hi]
@@ -441,8 +438,10 @@
 
     pltpu.make_async_copy(own_w, own_w, load_sem.at[1]).wait()
     pltpu.make_async_copy(own, own, load_sem.at[0]).wait()
-    pl.semaphore_wait(barrier, len(close))
+    lax.fori_loop(0, tiles, pack, 0)
+    pl.semaphore_wait(barrier, answers(close))
     tell(0)
+    tell(1)
 
     def send_lat(c):
         for side in range(2):
@@ -459,21 +458,21 @@
                     corner_copy(side, ew, c).start()
 
     send_lat(0)
-    lax.fori_loop(0, tiles, pack, 0)
     for ew in range(2):
         lon_copy(ew).start()
     hear(0)
-    tell(1)
     send_corners(0)
     send_lat(1)
     send_corners(1)
     lax.fori_loop(0, tiles, place_own, 0)
+    hear(1)
+    tell(2)
     for ew in range(2):
         lon_copy(ew).wait_recv()
     lax.fori_loop(0, tiles, place_lon, 0)
-    lax.fori_loop(0, ITERS // 2, two_levels(interior), 0)
-    hear(1)
-    tell(2)
+    interior()
+    hear(2)
+    tell(3)
     ready = ITERS // 2
     dots(0, ready, ((edge + HALF, edge + lat - HALF),))
     for c in range(2):
@@ -481,14 +480,16 @@
             place_halo(side, c)
         wedge(c)
         if c == 0:
-            hear(2)
-            tell(3)
+            hear(3)
+            tell(4)
             dots(0, ready, ((edge, edge + HALF), (edge + lat - HALF, edge + lat)))
             dots(ready + 1, ITERS, ((edge + HALF, edge + lat - HALF),))
             rim_dots(lambda p: ready + 1, lambda p: ready + p)
+            hear(4)
+            tell(5)
     rim_dots(lambda p: ready + 1 + p, lambda p: ITERS)
 
-    hear(3)
+    hear(5)
     sums = jnp.concatenate(
         [jnp.sum(gram_acc[n], axis=0, keepdims=True) for n in range(len(PAIRS))]
         + [jnp.zeros((128 - len(PAIRS), 128), f32)], axis=0)
@@ -600,7 +601,7 @@
                 pltpu.VMEM((nx * ny, 1, 128), f32),
                 dma((2,)),
                 dma((2,)), dma((2, 2)), dma((2,)), dma((2,)), dma((2,)),
-                pltpu.SemaphoreType.REGULAR((4,)),
+                pltpu.SemaphoreType.REGULAR((6,)),
             ],
             compiler_params=pltpu.CompilerParams(
                 collective_id=0, has_side_effects=True, vmem_limit_bytes=52_800_000),

time: 36.8 us -> 37.1 us (level)
  no operation moved by 1% of the time
where the time goes in v5:
time: 37.1 us; the launch traced here: 36.9 us
  Pallas kernels  36.1 us (97%)
  between operations  0.8 us (2%)
    pallas_call x1, Pallas kernels, per_device(): pl.pallas_call(functools.partial(kernel, nx, ny), out_shape=(pltpu.VMEM((...  33.9 us
    pallas_call x1, Pallas kernels, per_device(): pl.pallas_call(finish, out_shape=(shape, shape), in_specs=[vmem, vmem, vm...  2.16 us

profile of v5, /device:TPU:1, one launch (start us, length us, event | category | flops | bytes accessed | tf_op | source)
XLA Modules:
  0.0 36.9 jit_solution(3972578609628155585)
XLA Ops:
  0.6 33.9 %shard_map.68 = (f32[5,64,16,384]{3,2,1,0:T(8,128)S(1)}, f32[4,64,16,384]{3,2,1,0:T(8,128)S(1)}, f32[17,8,128]{2,1,0:T(8,128)S(1)}) custom-call(f32[16,32,256]{2,1,0:T(8,128)} %f_hbm.1, f32[16,32,256]{2,1,0:T(8,128)} %d_hbm.1, f32[16,16]{1,0:T(8,128)} %c_ref.1, f32[32,256]{1,0:T(8,128)} %wl_hbm.1, f32[32,256]{1,0:T(8,128)} %wa_hbm.1), custom_call_target="tpu_custom_call" | custom-call | tf_op jit(solution)/shard_map/pallas_call | solution.py:577
  34.6 2.2 %shard_map.69 = (f32[16,32,256]{2,1,0:T(8,128)}, f32[16,32,256]{2,1,0:T(8,128)}) custom-call(f32[5,64,16,384]{3,2,1,0:T(8,128)S(1)} %get-tuple-element.5.even, f32[4,64,16,384]{3,2,1,0:T(8,128)S(1)} %get-tuple-element.6.odd, f32[17,8,128]{2,1,0:T(8,128)S(1)} %get-tuple-element.7.splats), custom_call_target="tpu_custom_call" | custom-call | tf_op jit(solution)/shard_map/pallas_call | solution.py:609

commit v6 on v5

--- a/solution.py
+++ b/solution.py
@@ -478,10 +478,11 @@
     for c in range(2):
         for side in range(2):
             place_halo(side, c)
-        wedge(c)
         if c == 0:
             hear(3)
             tell(4)
+        wedge(c)
+        if c == 0:
             dots(0, ready, ((edge, edge + HALF), (edge + lat - HALF, edge + lat)))
             dots(ready + 1, ITERS, ((edge + HALF, edge + lat - HALF),))
             rim_dots(lambda p: ready + 1, lambda p: ready + p)

time: 37.1 us -> 37.3 us (level)
  no operation moved by 1% of the time
where the time goes in v6:
time: 37.3 us; the launch traced here: 37.1 us
  Pallas kernels  36.3 us (97%)
  between operations  0.8 us (2%)
    pallas_call x1, Pallas kernels, per_device(): pl.pallas_call(functools.partial(kernel, nx, ny), out_shape=(pltpu.VMEM((...  34.1 us
    pallas_call x1, Pallas kernels, per_device(): pl.pallas_call(finish, out_shape=(shape, shape), in_specs=[vmem, vmem, vm...  2.16 us

profile of v6, /device:TPU:1, one launch (start us, length us, event | category | flops | bytes accessed | tf_op | source)
XLA Modules:
  0.0 37.1 jit_solution(4391848094134473988)
XLA Ops:
  0.6 34.1 %shard_map.68 = (f32[5,64,16,384]{3,2,1,0:T(8,128)S(1)}, f32[4,64,16,384]{3,2,1,0:T(8,128)S(1)}, f32[17,8,128]{2,1,0:T(8,128)S(1)}) custom-call(f32[16,32,256]{2,1,0:T(8,128)} %f_hbm.1, f32[16,32,256]{2,1,0:T(8,128)} %d_hbm.1, f32[16,16]{1,0:T(8,128)} %c_ref.1, f32[32,256]{1,0:T(8,128)} %wl_hbm.1, f32[32,256]{1,0:T(8,128)} %wa_hbm.1), custom_call_target="tpu_custom_call" | custom-call | tf_op jit(solution)/shard_map/pallas_call | solution.py:578
  34.7 2.2 %shard_map.69 = (f32[16,32,256]{2,1,0:T(8,128)}, f32[16,32,256]{2,1,0:T(8,128)}) custom-call(f32[5,64,16,384]{3,2,1,0:T(8,128)S(1)} %get-tuple-element.5.even, f32[4,64,16,384]{3,2,1,0:T(8,128)S(1)} %get-tuple-element.6.odd, f32[17,8,128]{2,1,0:T(8,128)S(1)} %get-tuple-element.7.splats), custom_call_target="tpu_custom_call" | custom-call | tf_op jit(solution)/shard_map/pallas_call | solution.py:610

commit v7 on v5

--- a/solution.py
+++ b/solution.py
@@ -24,6 +24,7 @@
 GROUP = 4
 HALO = 2 * ITERS
 HALF = 8
+STEP = 4
 WINDOWS = 3
 
 
@@ -144,13 +145,8 @@
     def ring(n):
         return [(a, 0) for a in range(1, n + 1)] + [(nx - a, 0) for a in range(1, n + 1)]
 
-    def answers(offsets):
-        fixed = sum(1 for _, b in offsets if b == 0)
-        reach = max(b for _, b in offsets)
-        return fixed + jnp.minimum(ny - 1 - iy, reach) + jnp.minimum(iy, reach)
-
     close = line(1) + ring(1)
-    rounds = [line(1), ring(1), line(2) + ring(2), line(4), line(8), [(a, 0) for a in range(1, nx)]]
+    rounds = [line(1), ring(1), line(2) + ring(2), [(0, 4), (0, -4)], [(0, 8), (0, -8)], [(a, 0) for a in range(1, nx)]]
     for a, b in close:
         greet(barrier, a, b)
 
@@ -158,8 +154,15 @@
         for a, b in rounds[n]:
             greet(known.at[n], a, b)
 
+    def collect(sem, offsets):
+        count = sum(1 for _, b in offsets if b == 0)
+        for _, b in offsets:
+            if b > 0:
+                count = count + jnp.minimum(lax.div(ny - 1 - iy, b), 1) + jnp.minimum(lax.div(iy, b), 1)
+        pl.semaphore_wait(sem, count)
+
     def hear(n):
-        pl.semaphore_wait(known.at[n], answers(rounds[n]))
+        collect(known.at[n], rounds[n])
 
     winds = [pltpu.make_async_copy(wl_hbm, own_w.at[0], load_sem.at[1]), pltpu.make_async_copy(wa_hbm, own_w.at[1], load_sem.at[1])]
     for copy in winds:
@@ -208,28 +211,30 @@
         near_corner[3] = jnp.zeros(near_corner.shape[1:], f32)
 
     def lat_copies(side, c):
-        first = HALF * (1 - c) if side == 0 else HALF * c
+        first = HALO - STEP * (c + 1) if side == 0 else STEP * c
         base = lat - HALO if side == 0 else 0
         to = (ix, iy + 1) if side == 0 else (ix, iy - 1)
-        if c == 0:
-            parts = [(first, HALF, 0, both)]
+        if STEP * (c + 1) < HALO:
+            parts = [(first, STEP, both)]
         elif side == 0:
-            parts = [(first + 2, HALF - 2, 0, both), (first, 2, 0, channels)]
+            parts = [(first + 2, STEP - 2, both), (first, 2, channels)]
         else:
-            parts = [(first, HALF - 2, 0, both), (first + HALF - 2, 2, 0, channels)]
+            parts = [(first, STEP - 2, both), (first + STEP - 2, 2, channels)]
         out = []
-        for n, (start, count, sub, subs) in enumerate(parts):
+        for start, count, subs in parts:
             out.append(pltpu.make_async_remote_copy(
-                src_ref=own.at[pl.ds(base + start, count), pl.ds(sub, subs), :],
-                dst_ref=near_lat.at[side, pl.ds(start, count), pl.ds(sub, subs), :],
+                src_ref=own.at[pl.ds(base + start, count), pl.ds(0, subs), :],
+                dst_ref=near_lat.at[side, pl.ds(start, count), pl.ds(0, subs), :],
                 send_sem=lat_send.at[side], recv_sem=lat_recv.at[side, c], device_id=to, device_id_type=MESH))
-        out.append(pltpu.make_async_remote_copy(
-            src_ref=own_w.at[:, pl.ds(base + first, HALF), :], dst_ref=near_lat_w.at[side, :, pl.ds(first, HALF), :],
-            send_sem=lat_send.at[side], recv_sem=lat_recv.at[side, c], device_id=to, device_id_type=MESH))
+        if c % 2 == 0:
+            tile = tile_of(side, c)
+            out.append(pltpu.make_async_remote_copy(
+                src_ref=own_w.at[:, pl.ds(base + HALF * tile, HALF), :], dst_ref=near_lat_w.at[side, :, pl.ds(HALF * tile, HALF), :],
+                send_sem=lat_send.at[side], recv_sem=lat_recv.at[side, c], device_id=to, device_id_type=MESH))
         return out
 
     def tile_of(side, c):
-        return 1 - c if side == 0 else c
+        return 1 - c // 2 if side == 0 else c // 2
 
     def corner_copy(side, ew, c):
         slot, tile = 2 * side + ew, tile_of(side, c)
@@ -320,14 +325,19 @@
         return 0
 
     def place_halo(side, c):
-        first = HALF * (1 - c) if side == 0 else HALF * c
+        first = HALO - STEP * (c + 1) if side == 0 else STEP * c
         tile = tile_of(side, c)
-        e0 = first if side == 0 else edge + lat + first
+        shift = 0 if side == 0 else edge + lat
         inside = jnp.where(from_side(side), 1.0, 0.0).astype(f32)
 
         @pl.when(from_side(side))
         def _():
-            whole = diag.at[pl.ds(0, 13)] if c == 0 else coef.at[pl.ds(0, 35), :, pl.ds(0, 256)]
+            if c % 2 == 0:
+                whole = coef.at[pl.ds(0, 23), :, pl.ds(0, 256)]
+            elif STEP * (c + 1) < HALO:
+                whole = own.at[pl.ds(0, STEP)]
+            else:
+                whole = own.at[pl.ds(0, 3)]
             pltpu.make_async_copy(whole, whole, lat_recv.at[side, c]).wait()
 
         def three(a, b, w, e, lanes, at):
@@ -335,18 +345,19 @@
                     jnp.where(lanes >= 112, turn(e, 112 - at), turn(b, 112)))
 
         west_strip, east_strip = near_corner.at[2 * side, tile], near_corner.at[2 * side + 1, tile]
-        span = slice(first, first + 8)
-        wl, wa = (three(near_lat_w[side, q, span, 0:128], near_lat_w[side, q, span, 128:256],
-                        west_strip[both:both + 8, :], east_strip[both:both + 8, :], lane8, 16 * q) for q in range(2))
-        place_coef(e0, wl, wa, inside, range(WINDOWS))
-        for j in range(HALF):
-            middle = centre(e0 + j)
+        if c % 2 == 0:
+            span = slice(HALF * tile, HALF * tile + 8)
+            wl, wa = (three(near_lat_w[side, q, span, 0:128], near_lat_w[side, q, span, 128:256],
+                            west_strip[both:both + 8, :], east_strip[both:both + 8, :], lane8, 16 * q) for q in range(2))
+            place_coef(shift + HALF * tile, wl, wa, inside, range(WINDOWS))
+        for j in range(STEP):
+            middle = centre(shift + first + j)
             pieces = three(near_lat[side, first + j, :, 0:128], near_lat[side, first + j, :, 128:256],
-                           west_strip[0:both, :], east_strip[0:both, :], lane, 16 * j)
+                           west_strip[0:both, :], east_strip[0:both, :], lane, 16 * ((first + j) % HALF))
             for t, piece in enumerate(pieces):
                 cut = slice(128 * t, 128 * t + 128)
-                even[0, e0 + j, :, cut] = piece[0:channels]
-                diag[e0 + j, :, cut] = piece[channels:] * scale + middle
+                even[0, shift + first + j, :, cut] = piece[0:channels]
+                diag[shift + first + j, :, cut] = piece[channels:] * scale + middle
 
     def advance(level, start, count):
         src, dst, theta = field(level), field(level + 1), THETA[level] * scale
@@ -364,17 +375,18 @@
             moved.append(lax.dot_general(sides, band[...], (((1,), (0,)), ((), ())), preferred_element_type=f32))
         for g, picked in enumerate(groups):
             for j, e in enumerate(picked):
-                for t in range(WINDOWS):
-                    cut = slice(128 * t, 128 * t + 128)
-                    at = slice(size * t + channels * j, size * t + channels * (j + 1))
-
-                    def weight(q):
-                        return coef[e, q:q + 1, cut]
-
-                    value = (diag[e, :, cut] - theta) * src[e, :, cut] + mixed[g][channels * j:channels * (j + 1), cut]
-                    value = value + (coef[e, 0:1, 128:256] * moved[g][at, 0:128] + weight(1) * moved[g][at, 128:256])
-                    value = value + weight(2) * src[e + 1, :, cut] + weight(3) * src[e - 1, :, cut]
-                    dst[e, :, cut] = value + weight(4) * (src[e - 2, :, cut] - src[e + 2, :, cut])
+                at = [slice(size * t + channels * j, size * t + channels * (j + 1)) for t in range(WINDOWS)]
+                sums = jnp.concatenate([moved[g][a, 0:128] for a in at], axis=1)
+                slopes = jnp.concatenate([moved[g][a, 128:256] for a in at], axis=1)
+                kx = jnp.concatenate([coef[e, 0:1, 128:256]] * WINDOWS, axis=1)
+
+                def weight(q):
+                    return coef[e, q:q + 1, :]
+
+                value = (diag[e] - theta) * src[e] + mixed[g][channels * j:channels * (j + 1)]
+                value = value + (kx * sums + weight(1) * slopes)
+                value = value + weight(2) * src[e + 1] + weight(3) * src[e - 1]
+                dst[e] = value + weight(4) * (src[e - 2] - src[e + 2])
 
     def interior():
         for k in range(ITERS - 1):
@@ -384,62 +396,34 @@
 
     def wedge(c):
         for k in range(ITERS):
-            low = edge - HALF * (c + 1) + 2 + 2 * k
-            for e0 in (low, rows_all - HALF - low):
-                advance(k, e0, HALF // GROUP)
-
-    def dots(lo, hi, spans):
-        pairs = [(k, i) for k, i in PAIRS if lo <= k <= hi]
-
-        def one(t, _):
-            cut = pl.ds(pl.multiple_of(t * 128, 128), 128)
-            acc = (jnp.zeros((8, 128), f32),) * len(pairs)
-            for start, stop in spans:
-                def part(n, acc):
-                    acc = list(acc)
-                    for j in range(4):
-                        e = start + 4 * n + j
-                        for h in range(channels // 8):
-                            x = [field(k)[e, 8 * h:8 * h + 8, cut] for k in range(hi + 1)]
-                            for n_, (k, i) in enumerate(pairs):
-                                acc[n_] = acc[n_] + x[k] * x[i]
-                    return tuple(acc)
-
-                acc = lax.fori_loop(0, (stop - start) // 4, part, acc)
-            low = jnp.where(t == 1, 32, 16)
-            kept = (lane8 >= low) & (lane8 < 128 - low)
-            for n, (k, i) in enumerate(pairs):
-                at = k * (k + 1) // 2 + i
-                gram_acc[at] = gram_acc[at] + jnp.where(kept, acc[n], 0.0)
-            return 0
-
-        lax.fori_loop(0, WINDOWS, one, 0)
-
-    def rim_dots(first, last):
-        for t in range(WINDOWS):
-            cut = slice(128 * t, 128 * t + 128)
-            acc = {}
-            for p in range(HALF // 2):
-                for e in (edge + 2 * p, edge + 2 * p + 1, edge + lat - 1 - 2 * p, edge + lat - 2 - 2 * p):
-                    for h in range(channels // 8):
-                        levels = range(first(p), last(p) + 1)
-                        if not len(levels):
-                            continue
-                        x = [field(k)[e, 8 * h:8 * h + 8, cut] for k in range(last(p) + 1)]
-                        for k in levels:
-                            for i in range(k + 1):
-                                term = x[k] * x[i]
-                                acc[k, i] = acc[k, i] + term if (k, i) in acc else term
-            low = 32 if t == 1 else 16
-            kept = (lane8 >= low) & (lane8 < 128 - low)
-            for (k, i), value in acc.items():
-                at = k * (k + 1) // 2 + i
-                gram_acc[at] = gram_acc[at] + jnp.where(kept, value, 0.0)
+            low = edge - STEP * (c + 1) + 2 + 2 * k
+            for e0 in (low, rows_all - STEP - low):
+                advance(k, e0, STEP // GROUP)
+
+    def dots(c):
+        for k in range(ITERS + 1):
+            last = [p for p in range(lat // 4) if k <= p + 2 * (c + 1) and (c < 0 or k > p + 2 * c)]
+            pairs = [e for p in last for e in (edge + 2 * p, edge + lat - 2 - 2 * p)]
+            if not pairs:
+                continue
+            for group, low in (((0, 2), 16), ((1,), 32)):
+                acc = [None] * (k + 1)
+                for e in pairs:
+                    for t in group:
+                        x = [field(i)[e:e + 2, :, 128 * t:128 * t + 128] for i in range(k + 1)]
+                        for i in range(k + 1):
+                            term = x[k] * x[i]
+                            acc[i] = term if acc[i] is None else acc[i] + term
+                kept = (lane8 >= low) & (lane8 < 128 - low)
+                for i in range(k + 1):
+                    at = k * (k + 1) // 2 + i
+                    value = acc[i][0] + acc[i][1]
+                    gram_acc[at] = gram_acc[at] + jnp.where(kept, value[0:8] + value[8:16], 0.0)
 
     pltpu.make_async_copy(own_w, own_w, load_sem.at[1]).wait()
     pltpu.make_async_copy(own, own, load_sem.at[0]).wait()
     lax.fori_loop(0, tiles, pack, 0)
-    pl.semaphore_wait(barrier, answers(close))
+    collect(barrier, close)
     tell(0)
     tell(1)
 
@@ -463,7 +447,9 @@
     hear(0)
     send_corners(0)
     send_lat(1)
-    send_corners(1)
+    send_lat(2)
+    send_corners(2)
+    send_lat(3)
     lax.fori_loop(0, tiles, place_own, 0)
     hear(1)
     tell(2)
@@ -473,22 +459,18 @@
     interior()
     hear(2)
     tell(3)
-    ready = ITERS // 2
-    dots(0, ready, ((edge + HALF, edge + lat - HALF),))
-    for c in range(2):
+    dots(-1)
+    for c in range(HALO // STEP):
         for side in range(2):
             place_halo(side, c)
         wedge(c)
+        dots(c)
         if c == 0:
             hear(3)
             tell(4)
-            dots(0, ready, ((edge, edge + HALF), (edge + lat - HALF, edge + lat)))
-            dots(ready + 1, ITERS, ((edge + HALF, edge + lat - HALF),))
-            rim_dots(lambda p: ready + 1, lambda p: ready + p)
+        if c == 2:
             hear(4)
             tell(5)
-    rim_dots(lambda p: ready + 1 + p, lambda p: ITERS)
-
     hear(5)
     sums = jnp.concatenate(
         [jnp.sum(gram_acc[n], axis=0, keepdims=True) for n in range(len(PAIRS))]
@@ -600,7 +582,7 @@
                 pltpu.VMEM((1, 128), f32),
                 pltpu.VMEM((nx * ny, 1, 128), f32),
                 dma((2,)),
-                dma((2,)), dma((2, 2)), dma((2,)), dma((2,)), dma((2,)),
+                dma((2,)), dma((2, HALO // STEP)), dma((2,)), dma((2,)), dma((2,)),
                 pltpu.SemaphoreType.REGULAR((6,)),
             ],
             compiler_params=pltpu.CompilerParams(

time: 37.1 us -> 37 us (level)
  no operation moved by 1% of the time
where the time goes in v7:
time: 37 us; the launch traced here: 36.8 us
  Pallas kernels  36 us (97%)
  between operations  0.8 us (2%)
    pallas_call x1, Pallas kernels, per_device(): pl.pallas_call(functools.partial(kernel, nx, ny), out_shape=(pltpu.VMEM((...  33.8 us
    pallas_call x1, Pallas kernels, per_device(): pl.pallas_call(finish, out_shape=(shape, shape), in_specs=[vmem, vmem, vm...  2.16 us

profile of v7, /device:TPU:1, one launch (start us, length us, event | category | flops | bytes accessed | tf_op | source)
XLA Modules:
  0.0 36.8 jit_solution(7852750542842814195)
XLA Ops:
  0.6 33.8 %shard_map.68 = (f32[5,64,16,384]{3,2,1,0:T(8,128)S(1)}, f32[4,64,16,384]{3,2,1,0:T(8,128)S(1)}, f32[17,8,128]{2,1,0:T(8,128)S(1)}) custom-call(f32[16,32,256]{2,1,0:T(8,128)} %f_hbm.1, f32[16,32,256]{2,1,0:T(8,128)} %d_hbm.1, f32[16,16]{1,0:T(8,128)} %c_ref.1, f32[32,256]{1,0:T(8,128)} %wl_hbm.1, f32[32,256]{1,0:T(8,128)} %wa_hbm.1), custom_call_target="tpu_custom_call" | custom-call | tf_op jit(solution)/shard_map/pallas_call | solution.py:559
  34.5 2.2 %shard_map.69 = (f32[16,32,256]{2,1,0:T(8,128)}, f32[16,32,256]{2,1,0:T(8,128)}) custom-call(f32[5,64,16,384]{3,2,1,0:T(8,128)S(1)} %get-tuple-element.5.even, f32[4,64,16,384]{3,2,1,0:T(8,128)S(1)} %get-tuple-element.6.odd, f32[17,8,128]{2,1,0:T(8,128)S(1)} %get-tuple-element.7.splats), custom_call_target="tpu_custom_call" | custom-call | tf_op jit(solution)/shard_map/pallas_call | solution.py:591

commit v8 on v7

--- a/solution.py
+++ b/solution.py
@@ -171,44 +171,45 @@
         for q, src in enumerate((f_hbm, d_hbm)):
             pltpu.make_async_copy(src.at[c], own.at[:, q * channels + c, :], load_sem.at[0]).start()
 
-    def spread(n):
-        row = lax.broadcasted_iota(jnp.int32, (n, channels), 0)
-        col = lax.broadcasted_iota(jnp.int32, (n, channels), 1)
-        return jnp.where(lax.rem(row, channels) == col, 1.0, 0.0).astype(f32)
-
-    wide = lax.dot_general(spread(size), c_ref[...], (((1,), (0,)), ((), ())), precision=HI, preferred_element_type=f32)
-    wide = lax.dot_general(wide, spread(3 * size), (((1,), (1,)), ((), ())), precision=HI,
-                           preferred_element_type=f32) * (COUPLE * scale)
-    down = lax.broadcasted_iota(jnp.int32, (size, 3 * size), 0)
-    across = lax.broadcasted_iota(jnp.int32, (size, 3 * size), 1)
-    high = wide.astype(bf16).astype(f32)
-    wide = jnp.where(across < 2 * size, high, wide - high)
-    block[...] = jnp.where(down // channels == lax.rem(across, size) // channels, wide, 0.0).astype(bf16)
-    down = lax.broadcasted_iota(jnp.int32, (256, 256), 0)
-    across = lax.broadcasted_iota(jnp.int32, (256, 256), 1)
-    shift = lax.rem(down, 128) - lax.rem(across, 128)
-    sums = jnp.where((shift == 1) | (shift == -1), 1.0, 0.0)
-    slopes = jnp.where(shift == 1, 8.0, 0.0) + jnp.where(shift == -1, -8.0, 0.0)
-    slopes = slopes + jnp.where(shift == 2, -1.0, 0.0) + jnp.where(shift == -2, 1.0, 0.0)
-    band[...] = jnp.where(across < 128, sums, slopes).astype(bf16)
-    row_pos = (lax.broadcasted_iota(jnp.int32, (rows_all, 128), 0) + (iy * lat - edge)).astype(f32)
-    phi = -math.pi / 2 + (row_pos + 0.5) * (math.pi / (lat * ny))
-    kxs[...] = (DIFF_LON * scale) / (jnp.cos(phi) ** 2 + 0.1)
-    gram_acc[...] = jnp.zeros(gram_acc.shape, f32)
-
-    @pl.when(iy == 0)
-    def _():
-        near_lat[0] = jnp.zeros(near_lat.shape[1:], f32)
-        near_lat_w[0] = jnp.zeros(near_lat_w.shape[1:], f32)
-        near_corner[0] = jnp.zeros(near_corner.shape[1:], f32)
-        near_corner[1] = jnp.zeros(near_corner.shape[1:], f32)
-
-    @pl.when(iy == ny - 1)
-    def _():
-        near_lat[1] = jnp.zeros(near_lat.shape[1:], f32)
-        near_lat_w[1] = jnp.zeros(near_lat_w.shape[1:], f32)
-        near_corner[2] = jnp.zeros(near_corner.shape[1:], f32)
-        near_corner[3] = jnp.zeros(near_corner.shape[1:], f32)
+    def set_up():
+        def spread(n):
+            row = lax.broadcasted_iota(jnp.int32, (n, channels), 0)
+            col = lax.broadcasted_iota(jnp.int32, (n, channels), 1)
+            return jnp.where(lax.rem(row, channels) == col, 1.0, 0.0).astype(f32)
+
+        wide = lax.dot_general(spread(size), c_ref[...], (((1,), (0,)), ((), ())), precision=HI, preferred_element_type=f32)
+        wide = lax.dot_general(wide, spread(3 * size), (((1,), (1,)), ((), ())), precision=HI,
+                               preferred_element_type=f32) * (COUPLE * scale)
+        down = lax.broadcasted_iota(jnp.int32, (size, 3 * size), 0)
+        across = lax.broadcasted_iota(jnp.int32, (size, 3 * size), 1)
+        high = wide.astype(bf16).astype(f32)
+        wide = jnp.where(across < 2 * size, high, wide - high)
+        block[...] = jnp.where(down // channels == lax.rem(across, size) // channels, wide, 0.0).astype(bf16)
+        down = lax.broadcasted_iota(jnp.int32, (256, 256), 0)
+        across = lax.broadcasted_iota(jnp.int32, (256, 256), 1)
+        shift = lax.rem(down, 128) - lax.rem(across, 128)
+        sums = jnp.where((shift == 1) | (shift == -1), 1.0, 0.0)
+        slopes = jnp.where(shift == 1, 8.0, 0.0) + jnp.where(shift == -1, -8.0, 0.0)
+        slopes = slopes + jnp.where(shift == 2, -1.0, 0.0) + jnp.where(shift == -2, 1.0, 0.0)
+        band[...] = jnp.where(across < 128, sums, slopes).astype(bf16)
+        row_pos = (lax.broadcasted_iota(jnp.int32, (rows_all, 128), 0) + (iy * lat - edge)).astype(f32)
+        phi = -math.pi / 2 + (row_pos + 0.5) * (math.pi / (lat * ny))
+        kxs[...] = (DIFF_LON * scale) / (jnp.cos(phi) ** 2 + 0.1)
+        gram_acc[...] = jnp.zeros(gram_acc.shape, f32)
+
+        @pl.when(iy == 0)
+        def _():
+            near_lat[0] = jnp.zeros(near_lat.shape[1:], f32)
+            near_lat_w[0] = jnp.zeros(near_lat_w.shape[1:], f32)
+            near_corner[0] = jnp.zeros(near_corner.shape[1:], f32)
+            near_corner[1] = jnp.zeros(near_corner.shape[1:], f32)
+
+        @pl.when(iy == ny - 1)
+        def _():
+            near_lat[1] = jnp.zeros(near_lat.shape[1:], f32)
+            near_lat_w[1] = jnp.zeros(near_lat_w.shape[1:], f32)
+            near_corner[2] = jnp.zeros(near_corner.shape[1:], f32)
+            near_corner[3] = jnp.zeros(near_corner.shape[1:], f32)
 
     def lat_copies(side, c):
         first = HALO - STEP * (c + 1) if side == 0 else STEP * c
@@ -422,7 +423,6 @@
 
     pltpu.make_async_copy(own_w, own_w, load_sem.at[1]).wait()
     pltpu.make_async_copy(own, own, load_sem.at[0]).wait()
-    lax.fori_loop(0, tiles, pack, 0)
     collect(barrier, close)
     tell(0)
     tell(1)
@@ -442,8 +442,10 @@
                     corner_copy(side, ew, c).start()
 
     send_lat(0)
+    lax.fori_loop(0, tiles, pack, 0)
     for ew in range(2):
         lon_copy(ew).start()
+    set_up()
     hear(0)
     send_corners(0)
     send_lat(1)

time: 37 us -> 37 us (level)
  no operation moved by 1% of the time
where the time goes in v8:
time: 37 us; the launch traced here: 36.8 us
  Pallas kernels  36 us (97%)
  between operations  0.8 us (2%)
    pallas_call x1, Pallas kernels, per_device(): pl.pallas_call(functools.partial(kernel, nx, ny), out_shape=(pltpu.VMEM((...  33.8 us
    pallas_call x1, Pallas kernels, per_device(): pl.pallas_call(finish, out_shape=(shape, shape), in_specs=[vmem, vmem, vm...  2.16 us

profile of v8, /device:TPU:1, one launch (start us, length us, event | category | flops | bytes accessed | tf_op | source)
XLA Modules:
  0.0 36.8 jit_solution(6514327982003194541)
XLA Ops:
  0.6 33.8 %shard_map.68 = (f32[5,64,16,384]{3,2,1,0:T(8,128)S(1)}, f32[4,64,16,384]{3,2,1,0:T(8,128)S(1)}, f32[17,8,128]{2,1,0:T(8,128)S(1)}) custom-call(f32[16,32,256]{2,1,0:T(8,128)} %f_hbm.1, f32[16,32,256]{2,1,0:T(8,128)} %d_hbm.1, f32[16,16]{1,0:T(8,128)} %c_ref.1, f32[32,256]{1,0:T(8,128)} %wl_hbm.1, f32[32,256]{1,0:T(8,128)} %wa_hbm.1), custom_call_target="tpu_custom_call" | custom-call | tf_op jit(solution)/shard_map/pallas_call | solution.py:561
  34.5 2.2 %shard_map.69 = (f32[16,32,256]{2,1,0:T(8,128)}, f32[16,32,256]{2,1,0:T(8,128)}) custom-call(f32[5,64,16,384]{3,2,1,0:T(8,128)S(1)} %get-tuple-element.5.even, f32[4,64,16,384]{3,2,1,0:T(8,128)S(1)} %get-tuple-element.6.odd, f32[17,8,128]{2,1,0:T(8,128)S(1)} %get-tuple-element.7.splats), custom_call_target="tpu_custom_call" | custom-call | tf_op jit(solution)/shard_map/pallas_call | solution.py:593

commit v9 on v8

--- a/solution.py
+++ b/solution.py
@@ -182,9 +182,11 @@
                                preferred_element_type=f32) * (COUPLE * scale)
         down = lax.broadcasted_iota(jnp.int32, (size, 3 * size), 0)
         across = lax.broadcasted_iota(jnp.int32, (size, 3 * size), 1)
-        high = wide.astype(bf16).astype(f32)
-        wide = jnp.where(across < 2 * size, high, wide - high)
-        block[...] = jnp.where(down // channels == lax.rem(across, size) // channels, wide, 0.0).astype(bf16)
+        for k in range(ITERS):
+            moved = wide - jnp.where(lax.rem(across, size) == down, THETA[k] * scale, 0.0)
+            high = moved.astype(bf16).astype(f32)
+            moved = jnp.where(across < 2 * size, high, moved - high)
+            block[k] = jnp.where(down // channels == lax.rem(across, size) // channels, moved, 0.0).astype(bf16)
         down = lax.broadcasted_iota(jnp.int32, (256, 256), 0)
         across = lax.broadcasted_iota(jnp.int32, (256, 256), 1)
         shift = lax.rem(down, 128) - lax.rem(across, 128)
@@ -361,14 +363,14 @@
                 diag[shift + first + j, :, cut] = piece[channels:] * scale + middle
 
     def advance(level, start, count):
-        src, dst, theta = field(level), field(level + 1), THETA[level] * scale
+        src, dst = field(level), field(level + 1)
         groups = [[start + GROUP * g + j for j in range(GROUP)] for g in range(count)]
         mixed, moved = [], []
         for picked in groups:
             stack = jnp.concatenate([src[e] for e in picked], axis=0)
             high = stack.astype(bf16)
             low = (stack - high.astype(f32)).astype(bf16)
-            mixed.append(lax.dot_general(block[...], jnp.concatenate([high, low, high], axis=0), (((1,), (0,)), ((), ())),
+            mixed.append(lax.dot_general(block[level], jnp.concatenate([high, low, high], axis=0), (((1,), (0,)), ((), ())),
                                          preferred_element_type=f32))
             sides = jnp.concatenate(
                 [jnp.concatenate([high[:, 128 * t:128 * t + 128], low[:, 128 * t:128 * t + 128]], axis=1)
@@ -384,7 +386,7 @@
                 def weight(q):
                     return coef[e, q:q + 1, :]
 
-                value = (diag[e] - theta) * src[e] + mixed[g][channels * j:channels * (j + 1)]
+                value = diag[e] * src[e] + mixed[g][channels * j:channels * (j + 1)]
                 value = value + (kx * sums + weight(1) * slopes)
                 value = value + weight(2) * src[e + 1] + weight(3) * src[e - 1]
                 dst[e] = value + weight(4) * (src[e - 2] - src[e + 2])
@@ -571,7 +573,7 @@
                 pltpu.VMEM((rows_all, channels, lanes), f32),
                 pltpu.VMEM((rows_all, 8, lanes), f32),
                 pltpu.VMEM((rows_all, 128), f32),
-                pltpu.VMEM((GROUP * channels, 3 * GROUP * channels), jnp.bfloat16),
+                pltpu.VMEM((ITERS, GROUP * channels, 3 * GROUP * channels), jnp.bfloat16),
                 pltpu.VMEM((256, 256), jnp.bfloat16),
                 pltpu.VMEM((lat, 2 * channels, lon), f32),
                 pltpu.VMEM((2, HALO, 2 * channels, lon), f32),

time: 37 us -> 37 us (level)
  no operation moved by 1% of the time
where the time goes in v9:
time: 37 us; the launch traced here: 36.8 us
  Pallas kernels  36 us (97%)
  between operations  0.8 us (2%)
    pallas_call x1, Pallas kernels, per_device(): pl.pallas_call(functools.partial(kernel, nx, ny), out_shape=(pltpu.VMEM((...  33.8 us
    pallas_call x1, Pallas kernels, per_device(): pl.pallas_call(finish, out_shape=(shape, shape), in_specs=[vmem, vmem, vm...  2.16 us

profile of v9, /device:TPU:1, one launch (start us, length us, event | category | flops | bytes accessed | tf_op | source)
XLA Modules:
  0.0 36.8 jit_solution(8424869822722677877)
XLA Ops:
  0.6 33.8 %shard_map.68 = (f32[5,64,16,384]{3,2,1,0:T(8,128)S(1)}, f32[4,64,16,384]{3,2,1,0:T(8,128)S(1)}, f32[17,8,128]{2,1,0:T(8,128)S(1)}) custom-call(f32[16,32,256]{2,1,0:T(8,128)} %f_hbm.1, f32[16,32,256]{2,1,0:T(8,128)} %d_hbm.1, f32[16,16]{1,0:T(8,128)} %c_ref.1, f32[32,256]{1,0:T(8,128)} %wl_hbm.1, f32[32,256]{1,0:T(8,128)} %wa_hbm.1), custom_call_target="tpu_custom_call" | custom-call | tf_op jit(solution)/shard_map/pallas_call | solution.py:563
  34.4 2.2 %shard_map.69 = (f32[16,32,256]{2,1,0:T(8,128)}, f32[16,32,256]{2,1,0:T(8,128)}) custom-call(f32[5,64,16,384]{3,2,1,0:T(8,128)S(1)} %get-tuple-element.5.even, f32[4,64,16,384]{3,2,1,0:T(8,128)S(1)} %get-tuple-element.6.odd, f32[17,8,128]{2,1,0:T(8,128)S(1)} %get-tuple-element.7.splats), custom_call_target="tpu_custom_call" | custom-call | tf_op jit(solution)/shard_map/pallas_call | solution.py:595
